TPU v7x, 128 devices: a whole 4x4x4 slice. The times are simulated.
128 devices in a mesh: seq: 32 (over x, z, core), head: 4 (over y).
Axes of the slice: x: 4, y: 4, z: 4, core: 2. Of those that a mesh axis runs over, the one named last changes fastest.
Arguments:
- queries: bfloat16 [24576, 8192], P('seq', 'head'), may hold values from -6 to 6
- key_rows: bfloat16 [24576, 8192], P('seq', 'head'), may hold values from -0.5 to 0.5
- value_rows: bfloat16 [24576, 8192], P('seq', 'head'), may hold values from -130 to 130
- log_decay: float32 [64, 24576], P('head', 'seq'), may hold values from -1 to 0
- norm_gain: float32 [8192], P('head'), may hold values from 0.1 to 1.9
- grad_out: bfloat16 [24576, 8192], P('seq', 'head'), may hold values from -13 to 13
Outputs:
- output: bfloat16 [24576, 8192], P('seq', 'head')
- grad_queries: bfloat16 [24576, 8192], P('seq', 'head')
- grad_keys: bfloat16 [24576, 8192], P('seq', 'head')
- grad_values: bfloat16 [24576, 8192], P('seq', 'head')
- grad_gain: float32 [8192], P('head')
All inputs are finite; a program needn't handle non-finite values.
Results may differ from a plain program's by a relative error of at most 0.01.
Values sent between devices are 32-bit elements; how exact they have to be, the bound alone decides.
A program may use at most 192 MiB of HBM per device.

v0:
```python
import jax
import jax.numpy as jnp
from jax import lax
from jax.sharding import Mesh
from jax.sharding import PartitionSpec as P

DH = 128
HD = 8192
SEQ = ("seq_0", "seq_1", "seq_2")


EPSILON = 1e-06


def nothing_yet(x, identity):
    return jax.tree.map(
        lambda a, e: jnp.broadcast_to(jnp.asarray(e, a.dtype), a.shape), x, identity
    )


def prefix_by_axis(x, axes, combine, identity, reverse):
    before = start = nothing_yet(x, identity)
    so_far = x
    for axis in reversed(axes):
        count, place = (lax.axis_size(axis), lax.axis_index(axis))
        pieces = jax.tree.map(lambda part: lax.all_gather(part, axis), so_far)
        inside, so_far = (start, start)
        for k in reversed(range(count)) if reverse else range(count):
            passed = k > place if reverse else k < place
            so_far = combine(so_far, jax.tree.map(lambda part: part[k], pieces))
            inside = jax.tree.map(lambda new, old: jnp.where(passed, new, old), so_far, inside)
        before = combine(inside, before)
    return before


def from_everyone(x, axis):
    copies = jnp.broadcast_to(x, (lax.axis_size(axis), *x.shape))
    return lax.all_to_all(copies, axis, split_axis=0, concat_axis=0, tiled=True)


def over_copies(x, axis):
    everything = from_everyone(x, axis)
    return jnp.sum(everything, axis=0)


def in_one(arrays, axis):
    ends = [0]
    for a in arrays:
        ends.append(ends[-1] + a.size)
    so_far = over_copies(jnp.concatenate([a.ravel() for a in arrays]), axis)
    return tuple((so_far[b:e].reshape(a.shape) for a, b, e in zip(arrays, ends, ends[1:])))


def split_pair(operand):
    high = operand.astype(jnp.bfloat16)
    low = (operand - high.astype(jnp.float32)).astype(jnp.bfloat16)
    return (high, low)


def split_product(form, left, right):
    if left.dtype == jnp.float32:
        high, low = split_pair(left)
        return jnp.einsum(form, high, right, preferred_element_type=jnp.float32) + jnp.einsum(
            form, low, right, preferred_element_type=jnp.float32
        )
    if right.dtype == jnp.float32:
        high, low = split_pair(right)
        return jnp.einsum(form, left, high, preferred_element_type=jnp.float32) + jnp.einsum(
            form, left, low, preferred_element_type=jnp.float32
        )
    return jnp.einsum(form, left, right, preferred_element_type=jnp.float32)


def causal_decay(cumulative):
    length = cumulative.shape[-1]
    below_diag = jnp.arange(length)[:, None] >= jnp.arange(length)[None, :]
    spread = cumulative[..., :, None] - cumulative[..., None, :]
    return jnp.where(below_diag, jnp.exp(jnp.where(below_diag, spread, 0.0)), 0.0)


def split_heads(matrix):
    return matrix.reshape(matrix.shape[0], -1, DH).transpose(1, 0, 2)


def merge_heads(tensor):
    return tensor.transpose(1, 0, 2).reshape(tensor.shape[1], -1)


def affine_combine(earlier, later):
    return (earlier[0] * later[0], later[0][:, None, None] * earlier[1] + later[1])


def intra_forward(operands):
    q_head, k_head, v_head, cumul = operands
    decay_mask = causal_decay(cumul)
    scores = jnp.dot(q_head, k_head.T, preferred_element_type=jnp.float32)
    weights = (scores * decay_mask).astype(jnp.bfloat16)
    return jnp.dot(weights, v_head, preferred_element_type=jnp.float32)


def intra_backward(operands):
    q_head, k_head, v_head, grad_head, cumul = operands
    decay_mask = causal_decay(cumul)
    scores = jnp.dot(q_head, k_head.T, preferred_element_type=jnp.float32)
    weights = (scores * decay_mask).astype(jnp.bfloat16)
    grad_scores = jnp.dot(grad_head, v_head.T, preferred_element_type=jnp.float32)
    grad_weights = (grad_scores * decay_mask).astype(jnp.bfloat16)
    grad_q = jnp.dot(grad_weights, k_head, preferred_element_type=jnp.float32)
    grad_k = jnp.dot(grad_weights.T, q_head, preferred_element_type=jnp.float32)
    grad_v = jnp.dot(weights.T, grad_head, preferred_element_type=jnp.float32)
    return (grad_q, grad_k, grad_v)


def on_device(queries, key_rows, value_rows, log_decay, norm_gain, grad_out):
    q_heads = split_heads(queries)
    k_heads = split_heads(key_rows)
    v_heads = split_heads(value_rows)
    cumulative = jnp.cumsum(log_decay, axis=1)
    block_total = cumulative[:, -1]
    growth = jnp.exp(cumulative)[..., None]
    tail = jnp.exp(block_total[:, None] - cumulative)[..., None]
    decay_total = jnp.exp(block_total)
    local_state = split_product("htd,hte->hde", k_heads * tail, v_heads)
    identity = (jnp.ones_like(decay_total), jnp.zeros_like(local_state))
    state_in = prefix_by_axis((decay_total, local_state), SEQ, affine_combine, identity, False)[1]
    intra = lax.map(intra_forward, (q_heads, k_heads, v_heads, cumulative))
    attended = intra + growth * split_product("htd,hde->hte", q_heads, state_in)
    mixed = merge_heads(attended)
    scaled_grad = grad_out.astype(jnp.float32) * norm_gain[None, :]
    square_sum, cross_sum = in_one(
        (jnp.sum(mixed * mixed, axis=1), jnp.sum(scaled_grad * mixed, axis=1)), "head"
    )
    inverse = lax.rsqrt(square_sum / HD + EPSILON)
    normed = mixed * inverse[:, None]
    center = cross_sum * inverse / HD
    output = (normed * norm_gain[None, :]).astype(jnp.bfloat16)
    gain_part = jnp.sum(grad_out.astype(jnp.float32) * normed, axis=0)
    grad_gain = over_copies(gain_part, SEQ)
    grad_mixed = (inverse[:, None] * (scaled_grad - normed * center[:, None])).astype(jnp.bfloat16)
    grad_heads = split_heads(grad_mixed)
    state_grad = split_product("htd,hte->hde", q_heads * growth, grad_heads)
    identity = (jnp.ones_like(decay_total), jnp.zeros_like(state_grad))
    state_after = prefix_by_axis((decay_total, state_grad), SEQ, affine_combine, identity, True)[1]
    intra_q, intra_k, intra_v = lax.map(
        intra_backward, (q_heads, k_heads, v_heads, grad_heads, cumulative)
    )
    grad_q = intra_q + growth * split_product("hte,hde->htd", grad_heads, state_in)
    grad_k = intra_k + tail * split_product("hse,hde->hsd", v_heads, state_after)
    grad_v = intra_v + tail * split_product("hsd,hde->hse", k_heads, state_after)
    return (
        output,
        merge_heads(grad_q).astype(jnp.bfloat16),
        merge_heads(grad_k).astype(jnp.bfloat16),
        merge_heads(grad_v).astype(jnp.bfloat16),
        grad_gain,
    )


def solution(mesh):
    split = Mesh(
        mesh.devices.reshape(4, 4, 2, mesh.shape["head"]), ("seq_0", "seq_1", "seq_2", "head")
    )
    placed = (
        P(SEQ, "head"),
        P(SEQ, "head"),
        P(SEQ, "head"),
        P("head", SEQ),
        P("head"),
        P(SEQ, "head"),
    )
    return jax.shard_map(
        on_device,
        mesh=split,
        in_specs=placed,
        out_specs=(P(SEQ, "head"), P(SEQ, "head"), P(SEQ, "head"), P(SEQ, "head"), P("head")),
        check_vma=False,
    )
```

profile of v0, /device:TPU:1, one launch (start us, length us, event | category | flops | bytes accessed | tf_op | source)
XLA Modules:
  0.0 490.4 jit_solution(12226340317223105473)
XLA Ops:
  12.4 4.7 copy.136
  29.0 9.8 %all-reduce.1 = f32[64]{0:T(128)S(1)} all-reduce(f32[64]{0:T(128)S(1)} %multiply_dynamic-update-slice_fusion), channel_id=5, replica_groups=mesh['seq_0'=4,'seq_1'=4,'seq_2'=2,'head'=4] {'seq_1'}, use_global_device_ids=true, to_apply=%add.1 | all-reduce | flops 64 | bytes 512
  42.5 49.2 %all-gather.13.cloned.1.call-done = f32[4,16,128,128]{3,2,1,0:T(8,128)} async-done(((f32[1,16,128,128]{3,2,1,0:T(8,128)}), f32[4,16,128,128]{3,2,1,0:T(8,128)}) %all-gather.13.cloned.1.call-update) | async-done | bytes 4194320 | tf_op jit(solution)/shard_map/all_gather | solution.py:26
  98.1 4.7 copy.139
  102.7 4.7 copy.132
  107.5 4.7 copy.137
  112.2 8.9 %all-gather.4 = f32[4,1,16]{2,1,0:T(1,128)S(1)} all-gather(f32[1,1,16]{2,1,0:T(1,128)S(1)} %get-tuple-element.242), channel_id=1, replica_groups=mesh['seq_0'=4,'seq_1'=4,'seq_2'=2,'head'=4] {'seq_0'}, dimensions={0}, use_global_device_ids=true | all-gather | bytes 320 | tf_op jit(solution)/shard_map/all_gather | solution.py:26
  124.4 45.2 %while.24 = (s32[]{:T(128)}, f32[16,768,128]{1,2,0:T(8,128)}, bf16[16,768,128]{2,1,0:T(8,128)(2,1)}, bf16[16,768,128]{2,1,0:T(8,128)(2,1)}, f32[16,768]{1,0:T(8,...) while((s32[]{:T(128)}, f32[16,768,128]{1,2,0:T(8,128)}, bf16[16,768,128]{2,1,0:T(8,128)(2,1)}, ...), condition=%wide.region_3.4_spmd, body=%wide.region_2.3_spmd.sunk | while | flops 305528832 | bytes 999513 | solution.py:126
  169.7 5.4 %fusion.85 = f32[16,128,128]{2,1,0:T(8,128)S(1)} fusion(f32[4,16,128,128]{3,2,1,0:T(8,128)} %all-gather.15.cloned.1.call-done, f32[4,16,128,128]{3,2,1,0:T(8,128)} %all-gather.13.cloned.1.call-done, f32[32,128,128]{2,1,0:T(8,128)} %all-gather.21.cloned.1.call-done, f32[16]{0:T(128)S(1)} %get-tuple-element.243, f32[16]{0:T(128)S(1)} %get-tuple-element.246, ...), kind=kLoop, calls=%fused_computation.101 | loop fusion | flops 8126464 | bytes 11535114 | tf_op jit(solution)/shard_map/add | solution.py:90
  181.2 6.6 %copy.149 = f32[768,2048]{1,0:T(8,128)} copy(f32[768,2048]{0,1:T(8,128)} %bitcast.346) | data formatting | bytes 12582912 | tf_op jit(solution)/shard_map/reshape | solution.py:86
  192.4 8.1 %all_to_all.12 = f32[4,1,1536]{2,1,0:T(1,128)S(1)} all-to-all(f32[4,1,1536]{2,1,0:T(1,128)S(1)} %broadcast_in_dim.47), channel_id=1, replica_groups=mesh['seq_0'=4,'seq_1'=4,'seq_2'=2,'head'=4] {'head'}, dimensions={0} | all-to-all | bytes 49152 | tf_op jit(solution)/shard_map/all_to_all | solution.py:38
  200.5 6.4 %fusion.56 = (f32[2048]{0:T(1024)S(1)}, bf16[96,16,8,128]{3,2,1,0:T(8,128)(2,1)S(1)}, bf16[768,2048]{1,0:T(8,128)(2,1)}) fusion(bf16[768,2048]{1,0:T(8,128)(2,1)} %param.15, f32[768,2048]{1,0:T(8,128)} %copy.149, f32[768]{0:T(1024)S(1)} %get-tuple-element.232, f32[768]{0:T(1024)S(1)} %get-tuple-element.231, f32[2048]{0:T(1024)S(1)} %copy-done.12), kind=kLoop, calls=%fused_computation.58 | loop fusion | flops 17299456 | bytes 15751168 | tf_op jit(solution)/shard_map/reduce_sum | solution.py:137
  210.9 12.7 %all-gather.23.cloned.1.call-done = f32[32,128,128]{2,1,0:T(8,128)} async-done(((f32[16,128,128]{2,1,0:T(8,128)}), f32[32,128,128]{2,1,0:T(8,128)}) %all-gather.23.cloned.1.call-update) | async-done | bytes 2097168 | tf_op jit(solution)/shard_map/all_gather | solution.py:26
  226.4 8.0 %all-gather.5 = f32[4,1,16]{2,1,0:T(1,128)S(1)} all-gather(f32[1,1,16]{2,1,0:T(1,128)S(1)} %get-tuple-element.241), channel_id=1, replica_groups=mesh['seq_0'=4,'seq_1'=4,'seq_2'=2,'head'=4] {'seq_0'}, dimensions={0}, use_global_device_ids=true | all-gather | bytes 320 | tf_op jit(solution)/shard_map/all_gather | solution.py:26
  238.8 36.9 %all-gather.17.cloned.1.call-done = f32[4,16,128,128]{3,2,1,0:T(8,128)} async-done(((f32[1,16,128,128]{3,2,1,0:T(8,128)}), f32[4,16,128,128]{3,2,1,0:T(8,128)}) %all-gather.17.cloned.1.call-update) | async-done | bytes 4194320 | tf_op jit(solution)/shard_map/all_gather | solution.py:26
  289.1 137.4 %while.25 = (s32[]{:T(128)}, f32[16,768,128]{1,2,0:T(8,128)}, f32[16,768,128]{1,2,0:T(8,128)}, f32[16,768,128]{1,2,0:T(8,128)}, bf16[16,768,128]{2,1,0:T(8,128)(...) while((s32[]{:T(128)}, f32[16,768,128]{1,2,0:T(8,128)}, ...), condition=%wide.region_8.9_spmd, body=%wide.region_7.8_spmd.sunk | while | flops 762052608 | bytes 6122609 | solution.py:144
  427.4 6.7 %all-to-all-start.1 = ((f32[32,1,2048]{2,1,0:T(1,128)}), f32[32,1,2048]{2,1,0:T(1,128)S(1)}, u32[]{:S(2)}, u32[]{:S(2)}) async-start(f32[32,1,2048]{2,1,0:T(1,128)} %broadcast_in_dim.48), calls=%async_computation.1 | async-start | bytes 524288 | tf_op jit(solution)/shard_map/all_to_all | solution.py:38
  434.2 6.5 %fusion.112 = f32[16,768,128]{1,2,0:T(8,128)} fusion(f32[16,128,128]{2,1,0:T(8,128)} %copy-done.8, bf16[96,16,8,128]{3,2,1,0:T(8,128)(2,1)} %copy-done.4), kind=kOutput, calls=%fused_computation.185 | convolution fusion | flops 402915328 | bytes 10485760 | tf_op jit(solution)/shard_map/hte,hde->htd/dot_general | solution.py:68
  441.7 6.0 %add_convert_fusion = bf16[16,768,128]{1,2,0:T(8,128)(2,1)} fusion(f32[16,768,128]{1,2,0:T(8,128)S(1)} %copy-done.11, f32[16,768,128]{1,2,0:T(8,128)} %fusion.112, f32[16,768]{1,0:T(8,128)S(1)} %get-tuple-element.229, f32[16,128,128]{2,1,0:T(8,128)S(1)} %copy-done.9, bf16[96,16,8,128]{3,2,1,0:T(8,128)(2,1)S(1)} %copy-done.5), kind=kOutput, calls=%fused_computation.69 | convolution fusion | flops 409993216 | bytes 19972096 | tf_op jit(solution)/shard_map/hte,hde->htd/dot_general | solution.py:68
  447.8 4.6 copy.164
  453.3 5.4 %fusion.78 = f32[16,128,128]{2,1,0:T(8,128)S(1)} fusion(f32[4,16,128,128]{3,2,1,0:T(8,128)} %all-gather.19.cloned.1.call-done, f32[4,16,128,128]{3,2,1,0:T(8,128)} %all-gather.17.cloned.1.call-done, f32[32,128,128]{2,1,0:T(8,128)} %all-gather.23.cloned.1.call-done, f32[16]{0:T(128)S(1)} %copy-done.20, f32[16]{0:T(128)S(1)} %copy-done.22, ...), kind=kLoop, calls=%fused_computation.90 | loop fusion | flops 8126464 | bytes 11535114 | tf_op jit(solution)/shard_map/add | solution.py:90
  466.1 4.6 copy.165
  470.8 8.1 %fusion.57 = bf16[16,768,128]{1,2,0:T(8,128)(2,1)} fusion(f32[16,768,128]{1,2,0:T(8,128)} %get-tuple-element.89, f32[16,128,768]{2,1,0:T(8,128)} %fusion.108, f32[16,768]{1,0:T(8,128)S(1)} %get-tuple-element.230, bf16[16,768,128]{1,2,0:T(8,128)(2,1)S(1)} %bitcast.331, f32[16,128,128]{2,1,0:T(8,128)} %copy-done.10), kind=kOutput, calls=%fused_computation.60 | convolution fusion | flops 409993216 | bytes 19972096 | tf_op jit(solution)/shard_map/hsd,hde->hse/dot_general | solution.py:68
  478.9 4.6 copy.166
  (242 shorter events, 256.9 us)
Async XLA Ops:
  7.2 32.4 %all-gather.21.cloned.1.call-start = ((), (), s32[]{:S(2)}) async-start(), calls=%async_computation.6 | async-start | bytes 3145728 | tf_op jit(solution)/shard_map/all_gather | solution.py:26
  22.5 69.1 %all-gather.13.cloned.1.call-start = ((), (), s32[]{:S(2)}) async-start(), calls=%async_computation.2 | async-start | bytes 5242880 | tf_op jit(solution)/shard_map/all_gather | solution.py:26
  39.5 184.1 %copy-start.19 = (f32[16]{0:T(128)}, f32[16]{0:T(128)S(1)}, u32[]{:S(2)}) copy-start(f32[16]{0:T(128)S(1)} %get-tuple-element.244) | copy-start | bytes 196
  39.5 184.1 %copy-start.21 = (f32[16]{0:T(128)}, f32[16]{0:T(128)S(1)}, u32[]{:S(2)}) copy-start(f32[16]{0:T(128)S(1)} %get-tuple-element.245) | copy-start | bytes 196
  39.5 236.2 %copy-start.15 = (f32[16]{0:T(128)}, f32[16]{0:T(128)S(1)}, u32[]{:S(2)}) copy-start(f32[16]{0:T(128)S(1)} %get-tuple-element.249) | copy-start | bytes 196
  39.5 236.2 %copy-start.23 = (f32[16]{0:T(128)}, f32[16]{0:T(128)S(1)}, u32[]{:S(2)}) copy-start(f32[16]{0:T(128)S(1)} %get-tuple-element.248) | copy-start | bytes 196
  42.3 127.3 %all-gather.15.cloned.1.call-start = ((), (), s32[]{:S(2)}) async-start(), calls=%async_computation.3 | async-start | bytes 5242880 | tf_op jit(solution)/shard_map/all_gather | solution.py:26
  42.5 233.2 %copy-start.13 = (f32[16]{0:T(128)}, f32[16]{0:T(128)S(1)}, u32[]{:S(2)}) copy-start(f32[16]{0:T(128)S(1)} %get-tuple-element.251) | copy-start | bytes 196
  42.5 233.2 %copy-start.17 = (f32[16]{0:T(128)}, f32[16]{0:T(128)S(1)}, u32[]{:S(2)}) copy-start(f32[16]{0:T(128)S(1)} %get-tuple-element.250) | copy-start | bytes 196
  95.2 128.3 %all-gather.23.cloned.1.call-start = ((), (), s32[]{:S(2)}) async-start(), calls=%async_computation.7 | async-start | bytes 3145728 | tf_op jit(solution)/shard_map/all_gather | solution.py:26
  169.7 6.5 %slice-start.2 = ((s8[6291456]{0:T(1024)(128)(4,1)}), s8[4194304]{0:T(1024)(128)(4,1)S(1)}, s32[]{:S(2)}) async-start(s8[6291456]{0:T(1024)(128)(4,1)} %bitcast.344), calls=%async_computation.10 | async-start | bytes 8388608
  169.7 7.2 %slice-start.3 = ((s8[6291456]{0:T(1024)(128)(4,1)}), s8[2097152]{0:T(1024)(128)(4,1)S(1)}, s32[]{:S(2)}) async-start(s8[6291456]{0:T(1024)(128)(4,1)} %bitcast.344), calls=%async_computation.11 | async-start | bytes 4194304
  181.2 6.6 %copy-start.12 = (f32[2048]{0:T(1024)S(1)}, f32[2048]{0:T(1024)}, u32[]{:S(2)}) copy-start(f32[2048]{0:T(1024)} %param.14) | copy-start | bytes 24580
  200.5 6.4 %copy-start.7 = (bf16[768,2048]{0,1:T(8,128)(2,1)S(1)}, bf16[768,2048]{0,1:T(8,128)(2,1)}, u32[]{:S(2)}) copy-start(bf16[768,2048]{0,1:T(8,128)(2,1)} %copy.132) | copy-start | bytes 9437188
  210.8 64.9 %all-gather.17.cloned.1.call-start = ((), (), s32[]{:S(2)}) async-start(), calls=%async_computation.4 | async-start | bytes 5242880 | tf_op jit(solution)/shard_map/all_gather | solution.py:26
  226.4 226.9 %all-gather.19.cloned.1.call-start = ((), (), s32[]{:S(2)}) async-start(), calls=%async_computation.5 | async-start | bytes 5242880 | tf_op jit(solution)/shard_map/all_gather | solution.py:26
  427.4 25.1 %all-to-all-start.1 = ((f32[32,1,2048]{2,1,0:T(1,128)}), f32[32,1,2048]{2,1,0:T(1,128)S(1)}, u32[]{:S(2)}, u32[]{:S(2)}) async-start(f32[32,1,2048]{2,1,0:T(1,128)} %broadcast_in_dim.48), calls=%async_computation.1 | async-start | bytes 524288 | tf_op jit(solution)/shard_map/all_to_all | solution.py:38
  434.1 6.6 %copy-start.5 = (bf16[96,16,8,128]{3,2,1,0:T(8,128)(2,1)S(1)}, bf16[96,16,8,128]{3,2,1,0:T(8,128)(2,1)}, u32[]{:S(2)}) copy-start(bf16[96,16,8,128]{3,2,1,0:T(8,128)(2,1)} %copy-done.4) | copy-start | bytes 9437188
  434.1 6.6 %copy-start.9 = (f32[16,128,128]{2,1,0:T(8,128)S(1)}, f32[16,128,128]{2,1,0:T(8,128)}, u32[]{:S(2)}) copy-start(f32[16,128,128]{2,1,0:T(8,128)} %copy-done.8) | copy-start | bytes 3145732
  434.1 7.6 %copy-start.11 = (f32[16,768,128]{1,2,0:T(8,128)S(1)}, f32[16,768,128]{1,2,0:T(8,128)}, u32[]{:S(2)}) copy-start(f32[16,768,128]{1,2,0:T(8,128)} %get-tuple-element.87) | copy-start | bytes 18874372
  447.8 5.5 %copy-start.22 = (f32[16]{0:T(128)S(1)}, f32[16]{0:T(128)}, u32[]{:S(2)}) copy-start(f32[16]{0:T(128)} %copy-done.21) | copy-start | bytes 196
  447.8 5.5 %copy-start.24 = (f32[16]{0:T(128)S(1)}, f32[16]{0:T(128)}, u32[]{:S(2)}) copy-start(f32[16]{0:T(128)} %copy-done.23) | copy-start | bytes 196
  447.8 5.5 %copy-start.25 = (f32[16]{0:T(128)S(1)}, f32[16]{0:T(128)}, u32[]{:S(2)}) copy-start(f32[16]{0:T(128)} %get-tuple-element.222) | copy-start | bytes 196
  447.8 5.5 %copy-start.26 = (f32[16]{0:T(128)S(1)}, f32[16]{0:T(128)}, u32[]{:S(2)}) copy-start(f32[16]{0:T(128)} %get-tuple-element.223) | copy-start | bytes 196
  (16 other events, 64.2 us)
Sparse Core Ops, SparseCore 0:
  22.6 16.8 all-gather.20
  42.5 49.1 all-gather.12
  95.4 48.3 all-gather.14
  210.9 12.6 all-gather.22
  226.5 49.1 all-gather.16
  279.4 48.3 all-gather.18
where the time goes:
time: 493 us; the launch traced here: 490 us
  matrix products  224 us (45%)
  waiting for transfers between devices  99 us (20%)
  local copies, waits for them, and re-layouts  68.4 us (14%)
  blocking collectives  38.2 us (8%)
  other arithmetic  38 us (8%)
  between operations  15.9 us (3%)
  starting transfers between devices  6.98 us (1%)
    all_gather x6, waiting for transfers between devices, prefix_by_axis(): pieces = jax.tree.map(lambda part: lax.all_gather(part, axis), so_far)  98.9 us
    dot_general x16, matrix products, intra_forward(): return jnp.dot(weights, v_head, preferred_element_type=jnp.float32)  44.9 us
    dot_general x16, matrix products, intra_backward(): grad_v = jnp.dot(weights.T, grad_head, preferred_element_type=jnp.float32)  43.7 us
    dot_general x16, matrix products, intra_backward(): grad_q = jnp.dot(grad_weights, k_head, preferred_element_type=jnp.float32)  35.8 us
    dot_general x16, matrix products, intra_backward(): grad_k = jnp.dot(grad_weights.T, q_head, preferred_element_type=jnp.float32)  32.8 us
    unnamed x77, local copies, waits for them, and re-layouts  30.4 us
    dot_general x16, matrix products, intra_backward(): jnp.dot(grad_head, v_head.T, preferred_element_type=jnp.float32)  24.5 us
    add x6, other arithmetic, affine_combine(): later[0][:, None, None] * earlier[1] + later[1]  23.4 us
  transfers between devices with their start and end apart: 7, of which 4 were waited for; matrix products, arithmetic and copies ran while one was open for 49% of the time, Pallas kernels for 0%

commit v1 on v0

v1 whole, which is shorter than its diff:
```python
import functools

import jax
import jax.numpy as jnp
from jax import lax
from jax.experimental import pallas as pl
from jax.experimental.pallas import tpu as pltpu
from jax.sharding import PartitionSpec as P

DH = 128
EPSILON = 1e-06
F32 = jnp.float32
BF16 = jnp.bfloat16
MESH = pl.DeviceIdType.MESH
HIGHEST = lax.Precision.HIGHEST


def nn(a, b):
    return lax.dot_general(a, b, (((1,), (0,)), ((), ())), preferred_element_type=F32)


def nt(a, b):
    return lax.dot_general(a, b, (((1,), (1,)), ((), ())), preferred_element_type=F32)


def tn(a, b):
    return lax.dot_general(a, b, (((0,), (0,)), ((), ())), preferred_element_type=F32)


def exact_nt(a, b):
    return lax.dot_general(
        a, b, (((1,), (1,)), ((), ())), preferred_element_type=F32, precision=HIGHEST
    )


def kernel(
    sizes,
    q_in, k_in, v_in, ld, gain, g_in,
    out_hbm, gq_hbm, gk_hbm, gv_hbm, gg_out,
    q, k, v, g, cb, rc, ms, att, gvi, sbf, ga, qt,
    acc_s, acc_c, invb, cenb, sums, hx,
    dec_own, dec_par, dec_chip, dec_all,
    loc, lpr, tot, rx, px, pin, st, pst,
    gloc, glpr, gtot, grx, gpx, gpin, gst, gpst,
    ggp, ggpr, ggc, ggrx, ggsum, ggall,
    in_sem, out_sem, dp_s, dp_r, da_s, da_r, hx_s, hx_r,
    lp_s, lp_r, rx_s, rx_r, pi_s, pi_r, ps_s, ps_r,
    glp_s, glp_r, grx_s, grx_r, gpi_s, gpi_r, gps_s, gps_r,
    gp_s, gp_r, gr_s, gr_r, ga_s, ga_r,
):
    T, H, NC, NY = sizes
    NJ = T // DH
    HH = H // 2
    RS = HH * DH // NC
    HD = NY * H * DH
    me = lax.axis_index("seq")
    y = lax.axis_index("head")
    chip = me // 2
    core = me % 2
    mate = chip * 2 + (1 - core)
    own0 = core * HH
    oth0 = (1 - core) * HH

    def at(i):
        return {"seq": i * 2 + core}

    def remote(src, dst, s, r, dev):
        return pltpu.make_async_remote_copy(
            src_ref=src, dst_ref=dst, send_sem=s, recv_sem=r, device_id=dev, device_id_type=MESH
        )

    def loop(n, body):
        lax.fori_loop(0, n, lambda i, c: (body(i), c)[1], 0)

    def others(body):
        lax.fori_loop(1, NC, lambda r, c: (body(lax.rem(chip + r, NC)), c)[1], 0)

    loads = [
        pltpu.make_async_copy(src, dst, in_sem.at[n])
        for n, (src, dst) in enumerate(((k_in, k), (v_in, v), (q_in, q), (g_in, g)))
    ]
    for c in loads:
        c.start()

    barrier = pltpu.get_barrier_semaphore()
    others(
        lambda i: pl.semaphore_signal(barrier, inc=1, device_id=at(i), device_id_type=MESH)
    )
    pl.semaphore_signal(barrier, inc=1, device_id={"seq": mate}, device_id_type=MESH)
    for r in range(1, NY):
        pl.semaphore_signal(
            barrier, inc=1, device_id={"head": lax.rem(y + r, NY)}, device_id_type=MESH
        )

    row_i = lax.broadcasted_iota(jnp.int32, (DH, DH), 0)
    col_i = lax.broadcasted_iota(jnp.int32, (DH, DH), 1)
    lower = row_i >= col_i
    upper = row_i <= col_i
    tri = jnp.where(lower, 1.0, 0.0).astype(F32)

    total = jnp.zeros((H, 1), F32)
    for j in range(NJ):
        piece = ld[:, j * DH:(j + 1) * DH]
        rows = exact_nt(piece, tri)
        columns = exact_nt(tri, piece)
        for h in range(H):
            rc[h, :, j * DH:(j + 1) * DH] = rows[h:h + 1, :]
            cb[h, j * DH:(j + 1) * DH, :] = jnp.broadcast_to(columns[:, h:h + 1], (DH, DH))
        total = total + rows[:, DH - 1:DH]
    dec_own[...] = jnp.broadcast_to(total, (H, DH)).reshape(H, 1, DH)

    pl.semaphore_wait(barrier, NC - 1 + 1 + NY - 1)
    dec_copy = remote(dec_own, dec_par, dp_s.at[0], dp_r.at[0], {"seq": mate})
    dec_copy.start()

    def tile(ref, h, j):
        return ref[j * DH:(j + 1) * DH, pl.ds(pl.multiple_of(h * DH, DH), DH)]

    def put(ref, h, j, value):
        ref[j * DH:(j + 1) * DH, pl.ds(pl.multiple_of(h * DH, DH), DH)] = value

    def cums(h, j):
        return cb[h, j * DH:(j + 1) * DH, :]

    def cum_row(h, j):
        return rc[h, :, j * DH:(j + 1) * DH]

    def local_states(h):
        state = None
        for j in range(NJ):
            cum = cums(h, j)
            end = cum[DH - 1:DH, :]
            scaled = (tile(k, h, j).astype(F32) * jnp.exp(end - cum)).astype(BF16)
            part = tn(scaled, tile(v, h, j))
            ms[h, j] = part
            state = part if state is None else jnp.exp(end) * state + part
        loc[h] = state

    def to_mate(src, dst, s, r, n):
        return remote(src, dst, s.at[n], r.at[n], {"seq": mate})

    def scan_total(first, src, recv, dst):
        def one(r):
            h = own0 + r
            mine = jnp.where(first, jnp.exp(dec_par[h]), 1.0)
            theirs = jnp.where(first, 1.0, jnp.exp(dec_own[h]))
            dst[pl.ds(pl.multiple_of(r * DH, DH), DH), :] = mine * src[h] + theirs * recv[r]

        loop(HH, one)

    def piece_of(ref, i):
        return ref.at[pl.ds(pl.multiple_of(i * RS, RS), RS), :]

    def out_copy(src, dst, s, r, i):
        return remote(piece_of(src, i), dst.at[chip], s.at[i], r.at[chip], at(i))

    def in_copy(src, dst, s, r, i):
        return remote(piece_of(src, i), dst.at[i], s.at[i], r.at[i], at(i))

    def back_copy(src, dst, s, r, i):
        return remote(src.at[i], piece_of(dst, chip), s.at[i], r.at[chip], at(i))

    def home_copy(src, dst, s, r, i):
        return remote(src.at[i], piece_of(dst, i), s.at[i], r.at[i], at(i))

    def prefix(src, recv, dst, s, r, reverse):
        head = own0 + (chip * RS) // DH
        recv[chip] = src[pl.ds(pl.multiple_of(chip * RS, RS), RS), :]

        def one(n, state):
            i = NC - 1 - n if reverse else n

            @pl.when(i != chip)
            def _():
                in_copy(src, recv, s, r, i).wait_recv()

            dst[i] = state
            return jnp.exp(dec_all[i, head]) * state + recv[i]

        lax.fori_loop(0, NC, one, jnp.zeros((RS, DH), F32))

    def settle(first, homed, local, recv, dst, out):
        def one(r):
            h = own0 + r
            state = homed[pl.ds(pl.multiple_of(r * DH, DH), DH), :]
            ahead = jnp.where(first, 1.0, jnp.exp(dec_par[h]))
            dst[h] = ahead * state + jnp.where(first, 0.0, recv[r])
            after = jnp.where(first, jnp.exp(dec_own[h]), 1.0)
            out[r] = after * state + jnp.where(first, local[h], 0.0)

        loop(HH, one)

    loads[0].wait()
    loads[1].wait()

    def first_half(r):
        local_states(oth0 + r)
        to_mate(loc.at[oth0 + r], lpr.at[r], lp_s, lp_r, r).start()

    loop(HH, first_half)
    dec_copy.wait()
    dec_chip[...] = dec_own[...] + dec_par[...]
    dec_all[chip] = dec_chip[...]
    others(lambda i: remote(dec_chip, dec_all.at[chip], da_s.at[i], da_r.at[chip], at(i)).start())
    loop(HH, lambda r: local_states(own0 + r))
    loop(HH, lambda r: to_mate(loc.at[oth0 + r], lpr.at[r], lp_s, lp_r, r).wait())
    scan_total(core == 0, loc, lpr, tot)
    others(lambda i: out_copy(tot, rx, rx_s, rx_r, i).start())

    loads[2].wait()

    def intra(h):
        for j in range(NJ):
            qj = tile(q, h, j)
            decay = jnp.exp(jnp.where(lower, cums(h, j) - cum_row(h, j), -jnp.inf))
            weights = (nt(qj, tile(k, h, j)) * decay).astype(BF16)
            put(att, h, j, nn(weights, tile(v, h, j)))
            qt[h, :, j * DH:(j + 1) * DH] = qj.T

    loop(HH, intra)
    others(lambda i: remote(dec_chip, dec_all.at[i], da_s.at[i], da_r.at[i], at(i)).wait())
    prefix(tot, rx, px, rx_s, rx_r, False)
    others(lambda i: back_copy(px, pin, pi_s, pi_r, i).start())
    pin[pl.ds(pl.multiple_of(chip * RS, RS), RS), :] = px[chip]
    loop(HH, lambda r: intra(HH + r))
    loads[3].wait()
    acc_s[...] = jnp.zeros_like(acc_s)
    acc_c[...] = jnp.zeros_like(acc_c)
    others(lambda i: home_copy(px, pin, pi_s, pi_r, i).wait_recv())
    settle(core == 0, pin, loc, lpr, st, pst)
    loop(HH, lambda r: to_mate(pst.at[r], st.at[own0 + r], ps_s, ps_r, r).start())

    def inter(h):
        state = st[h]
        scale = gain[:, pl.ds(pl.multiple_of(h * DH, DH), DH)]
        for j in range(NJ):
            cum = cums(h, j)
            low = state.astype(BF16)
            sbf[h, j] = low
            mixed = tile(att, h, j) + jnp.exp(cum) * nn(tile(q, h, j), low)
            put(att, h, j, mixed)
            acc_s[j * DH:(j + 1) * DH, :] += mixed * mixed
            acc_c[j * DH:(j + 1) * DH, :] += tile(g, h, j).astype(F32) * scale * mixed
            if j < NJ - 1:
                state = jnp.exp(cum[DH - 1:DH, :]) * state + ms[h, j]

    loop(HH, lambda r: inter(own0 + r))

    def second_half(r):
        to_mate(pst.at[r], st.at[oth0 + r], ps_s, ps_r, r).wait_recv()
        inter(oth0 + r)

    loop(HH, second_half)

    ones = jnp.ones((8, DH), F32)
    pick = lax.broadcasted_iota(jnp.int32, (8, DH), 0) == 0
    for j in range(NJ):
        a = exact_nt(ones, acc_s[j * DH:(j + 1) * DH, :])
        b = exact_nt(ones, acc_c[j * DH:(j + 1) * DH, :])
        sums[:, j * DH:(j + 1) * DH] = jnp.where(pick, a, b)
    for r in range(1, NY):
        d = lax.rem(y + r, NY)
        remote(sums, hx.at[y], hx_s.at[d], hx_r.at[y], {"head": d}).start()
    hx[y] = sums[...]
    for r in range(1, NY):
        d = lax.rem(y + r, NY)
        remote(sums, hx.at[d], hx_s.at[d], hx_r.at[d], {"head": d}).wait()
    for j in range(NJ):
        both = hx[0, :, j * DH:(j + 1) * DH]
        for r in range(1, NY):
            both = both + hx[r, :, j * DH:(j + 1) * DH]
        both = both.T
        inverse = lax.rsqrt(both[:, 0:1] / HD + EPSILON)
        center = both[:, 1:2] * inverse / HD
        invb[j * DH:(j + 1) * DH, :] = jnp.broadcast_to(inverse, (DH, DH))
        cenb[j * DH:(j + 1) * DH, :] = jnp.broadcast_to(center, (DH, DH))

    def normalize(h):
        scale = gain[:, pl.ds(pl.multiple_of(h * DH, DH), DH)]
        gain_part = jnp.zeros((8, DH), F32)
        for j in range(NJ):
            inverse = invb[j * DH:(j + 1) * DH, :]
            normed = tile(att, h, j) * inverse
            grad = tile(g, h, j).astype(F32)
            put(g, h, j, (normed * scale).astype(BF16))
            gain_part = gain_part + jnp.sum((grad * normed).reshape(DH // 8, 8, DH), axis=0)
            center = cenb[j * DH:(j + 1) * DH, :]
            low = (inverse * (grad * scale - normed * center)).astype(BF16)
            put(ga, h, j, low)
            lifted = qt[h, :, j * DH:(j + 1) * DH].astype(F32) * jnp.exp(cum_row(h, j))
            ms[h, j] = nn(lifted.astype(BF16), low)
        ggp[h] = gain_part
        state = ms[h, NJ - 1]
        for j in range(NJ - 2, -1, -1):
            end = cb[h, j * DH + DH - 1:j * DH + DH, :]
            state = jnp.exp(end) * state + ms[h, j]
        gloc[h] = state

    def normalize_send(r):
        normalize(oth0 + r)
        to_mate(gloc.at[oth0 + r], glpr.at[r], glp_s, glp_r, r).start()

    loop(HH, normalize_send)
    loop(HH, lambda r: normalize(own0 + r))
    gain_copy = to_mate(ggp, ggpr, gp_s, gp_r, 0)
    gain_copy.start()
    store_out = pltpu.make_async_copy(g, out_hbm, out_sem.at[0])
    store_out.start()
    loop(HH, lambda r: to_mate(gloc.at[oth0 + r], glpr.at[r], glp_s, glp_r, r).wait())
    scan_total(core == 1, gloc, glpr, gtot)
    others(lambda i: out_copy(gtot, grx, grx_s, grx_r, i).start())
    gain_copy.wait()
    ggc[...] = ggp[...] + ggpr[...]
    others(lambda i: remote(ggc.at[i], ggrx.at[chip], gr_s.at[i], gr_r.at[chip], at(i)).start())
    ggrx[chip] = ggc[chip]

    def intra_grads(h):
        for j in range(NJ):
            qj, kj, vj, gj = (tile(ref, h, j) for ref in (q, k, v, ga))
            cum = cums(h, j)
            row = cum_row(h, j)
            decay = jnp.exp(jnp.where(lower, cum - row, -jnp.inf))
            flipped = jnp.exp(jnp.where(upper, row - cum, -jnp.inf))
            gw = (nt(gj, vj) * decay).astype(BF16)
            gwt = (nt(vj, gj) * flipped).astype(BF16)
            wt = (nt(kj, qj) * flipped).astype(BF16)
            gq = nn(gw, kj) + jnp.exp(cum) * nt(gj, sbf[h, j])
            put(att, h, j, nn(gwt, qj))
            put(gvi, h, j, nn(wt, gj))
            put(q, h, j, gq.astype(BF16))

    loop(HH, intra_grads)
    prefix(gtot, grx, gpx, grx_s, grx_r, True)
    others(lambda i: back_copy(gpx, gpin, gpi_s, gpi_r, i).start())
    gpin[pl.ds(pl.multiple_of(chip * RS, RS), RS), :] = gpx[chip]
    others(lambda i: remote(ggc.at[i], ggrx.at[i], gr_s.at[i], gr_r.at[i], at(i)).wait())
    part = ggrx[0]
    for i in range(1, NC):
        part = part + ggrx[i]
    ggsum[...] = part
    others(lambda i: remote(ggsum, ggall.at[chip], ga_s.at[i], ga_r.at[chip], at(i)).start())
    ggall[chip] = part
    loop(HH, lambda r: intra_grads(HH + r))
    store_q = pltpu.make_async_copy(q, gq_hbm, out_sem.at[1])
    store_q.start()
    others(lambda i: home_copy(gpx, gpin, gpi_s, gpi_r, i).wait_recv())
    settle(core == 1, gpin, gloc, glpr, gst, gpst)
    loop(HH, lambda r: to_mate(gpst.at[r], gst.at[own0 + r], gps_s, gps_r, r).start())

    def inter_grads(h):
        state = gst[h]
        for j in range(NJ - 1, -1, -1):
            cum = cums(h, j)
            end = cum[DH - 1:DH, :]
            low = state.astype(BF16)
            tail = jnp.exp(end - cum)
            kj, vj = tile(k, h, j), tile(v, h, j)
            gk = tile(att, h, j) + tail * nt(vj, low)
            gv = tile(gvi, h, j) + tail * nn(kj, low)
            put(k, h, j, gk.astype(BF16))
            put(v, h, j, gv.astype(BF16))
            if j > 0:
                state = jnp.exp(end) * state + ms[h, j]

    loop(HH, lambda r: inter_grads(own0 + r))

    def grads_half(r):
        to_mate(gpst.at[r], gst.at[oth0 + r], gps_s, gps_r, r).wait_recv()
        inter_grads(oth0 + r)

    loop(HH, grads_half)
    store_k = pltpu.make_async_copy(k, gk_hbm, out_sem.at[2])
    store_k.start()
    store_v = pltpu.make_async_copy(v, gv_hbm, out_sem.at[3])
    store_v.start()
    others(lambda i: remote(ggsum, ggall.at[i], ga_s.at[i], ga_r.at[i], at(i)).wait())
    for h in range(H):
        gg_out[h:h + 1, :] = jnp.sum(ggall[h], axis=0, keepdims=True)

    others(lambda i: in_copy(tot, rx, rx_s, rx_r, i).wait_send())
    others(lambda i: home_copy(px, pin, pi_s, pi_r, i).wait_send())
    others(lambda i: in_copy(gtot, grx, grx_s, grx_r, i).wait_send())
    others(lambda i: home_copy(gpx, gpin, gpi_s, gpi_r, i).wait_send())
    loop(HH, lambda r: to_mate(pst.at[r], st.at[oth0 + r], ps_s, ps_r, r).wait_send())
    loop(HH, lambda r: to_mate(gpst.at[r], gst.at[oth0 + r], gps_s, gps_r, r).wait_send())
    for c in (store_out, store_q, store_k, store_v):
        c.wait()


def on_device(sizes, queries, key_rows, value_rows, log_decay, norm_gain, grad_out):
    T, H, NC, NY = sizes
    W = H * DH
    NJ = T // DH
    HH = H // 2
    RS = HH * DH // NC
    V = pltpu.VMEM
    D = pltpu.SemaphoreType.DMA
    mate_scan = [
        V((H, DH, DH), F32), V((HH, DH, DH), F32), V((HH * DH, DH), F32), V((NC, RS, DH), F32),
        V((NC, RS, DH), F32), V((HH * DH, DH), F32), V((H, DH, DH), F32), V((HH, DH, DH), F32),
    ]
    scan_sems = [D((HH,)), D((HH,)), D((NC,)), D((NC,)), D((NC,)), D((NC,)), D((HH,)), D((HH,))]
    scratch = [
        V((T, W), BF16), V((T, W), BF16), V((T, W), BF16), V((T, W), BF16),
        V((H, T, DH), F32), V((H, 1, T), F32), V((H, NJ, DH, DH), F32), V((T, W), F32),
        V((T, W), F32), V((H, NJ, DH, DH), BF16), V((T, W), BF16), V((H, DH, T), BF16),
        V((T, DH), F32), V((T, DH), F32), V((T, DH), F32), V((T, DH), F32),
        V((8, T), F32), V((NY, 8, T), F32),
        V((H, 1, DH), F32), V((H, 1, DH), F32), V((H, 1, DH), F32), V((NC, H, 1, DH), F32),
        *mate_scan, *mate_scan,
        V((H, 8, DH), F32), V((H, 8, DH), F32), V((H, 8, DH), F32), V((NC, 8, DH), F32),
        V((8, DH), F32), V((NC, 8, DH), F32),
        D((4,)), D((4,)), D((1,)), D((1,)), D((NC,)), D((NC,)), D((NY,)), D((NY,)),
        *scan_sems, *scan_sems,
        D((1,)), D((1,)), D((NC,)), D((NC,)), D((NC,)), D((NC,)),
    ]
    big = jax.ShapeDtypeStruct((T, W), BF16)
    anywhere = pl.BlockSpec(memory_space=pl.ANY)
    local = pl.BlockSpec(memory_space=pltpu.VMEM)
    *grads, gain_grad = pl.pallas_call(
        functools.partial(kernel, sizes),
        out_shape=(big, big, big, big, jax.ShapeDtypeStruct((H, DH), F32)),
        in_specs=[anywhere, anywhere, anywhere, local, local, anywhere],
        out_specs=(anywhere, anywhere, anywhere, anywhere, local),
        scratch_shapes=scratch,
        compiler_params=pltpu.CompilerParams(
            collective_id=0, has_side_effects=True, vmem_limit_bytes=66_000_000
        ),
    )(queries, key_rows, value_rows, log_decay, norm_gain.reshape(1, W), grad_out)
    return (*grads, gain_grad.reshape(W))


def solution(mesh):
    def whole(queries, key_rows, value_rows, log_decay, norm_gain, grad_out):
        seq, head = mesh.shape["seq"], mesh.shape["head"]
        sizes = (queries.shape[0] // seq, queries.shape[1] // DH // head, seq // 2, head)
        rows = P("seq", "head")
        return jax.shard_map(
            functools.partial(on_device, sizes),
            mesh=mesh,
            in_specs=(rows, rows, rows, P("head", "seq"), P("head"), rows),
            out_specs=(rows, rows, rows, rows, P("head")),
            check_vma=False,
        )(queries, key_rows, value_rows, log_decay, norm_gain, grad_out)

    return whole
```

time: 493 us -> 96.4 us (0.20)
  matrix products: 224 us -> 0 us
  waiting for transfers between devices: 99 us -> 0 us
  Pallas kernels: 0 us -> 83 us
  local copies, waits for them, and re-layouts: 68.4 us -> 12.4 us
  blocking collectives: 38.2 us -> 0 us
  other arithmetic: 38 us -> 0 us
  between operations: 15.9 us -> 0.65 us
  starting transfers between devices: 6.98 us -> 0 us
    dot_general x92 -> x0, matrix products: 224 us -> none  [the longest x16 44.9 us: intra_forward(): return jnp.dot(weights, v_head, preferred_element_type=jnp.float32)]
    all_gather x6 -> x0, waiting for transfers between devices: 98.9 us -> none  [prefix_by_axis(): pieces = jax.tree.map(lambda part: lax.all_gather(part, axis), so_far)]
    pallas_call x0 -> x1, Pallas kernels: none -> 83 us  [on_device(): pl.pallas_call(functools.partial(kernel, sizes), out_shape=(big, big, big...]
    add x6 -> x0, other arithmetic: 23.4 us -> none  [affine_combine(): later[0][:, None, None] * earlier[1] + later[1]]
    unnamed x77 -> x13, local copies, waits for them, and re-layouts: 30.4 us -> 12.4 us
    all_gather x2 -> x0, blocking collectives: 16.8 us -> none  [prefix_by_axis(): pieces = jax.tree.map(lambda part: lax.all_gather(part, axis), so_far)]
    unnamed x2 -> x0, blocking collectives: 13.3 us -> none
    another operation x4 -> x0, local copies, waits for them, and re-layouts: 13.1 us -> none
  transfers between devices with their start and end apart: 7 -> 0, of which waited for: 4 -> 0; matrix products, arithmetic and copies ran while one was open for 49% -> 0% of each run, Pallas kernels for 0% -> 0%
where the time goes in v1:
time: 96.4 us; the launch traced here: 96.1 us
  Pallas kernels  83 us (86%)
  local copies, waits for them, and re-layouts  12.4 us (13%)
    pallas_call x1, Pallas kernels, on_device(): pl.pallas_call(functools.partial(kernel, sizes), out_shape=(big, big, big...  83 us
    unnamed x13, local copies, waits for them, and re-layouts  12.4 us

profile of v1, /device:TPU:1, one launch (start us, length us, event | category | flops | bytes accessed | tf_op | source)
XLA Modules:
  0.0 96.1 jit_solution(5841756216017893241)
XLA Ops:
  0.6 83.0 %shard_map.101 = (bf16[768,2048]{1,0:T(8,128)(2,1)}, bf16[768,2048]{1,0:T(8,128)(2,1)}, bf16[768,2048]{1,0:T(8,128)(2,1)}, bf16[768,2048]{1,0:T(8,128)(2,1)}, f32[16,128]{1,0:T(8,128)}) custom-call(bf16[768,2048]{1,0:T(8,128)(2,1)} %q_in.1, bf16[768,2048]{1,0:T(8,128)(2,1)} %k_in.1, bf16[768,2048]{1,0:T(8,128)(2,1)} %v_in.1, f32[16,768]{1,0:T(8,128)} %ld.1, ...), custom_call_target="tpu_custom_call" | custom-call | tf_op jit(solution)/shard_map/pallas_call | solution.py:420
  83.7 0.0 copy-start.2
  83.7 4.1 %copy.16 = bf16[768,2048]{1,0:T(8,128)(2,1)} copy(bf16[768,2048]{1,0:T(8,128)(2,1)} %get-tuple-element.20) | data formatting | bytes 6291456
  87.8 0.0 copy-done.2
  87.8 0.0 copy-start.1
  87.8 1.7 %copy.17 = bf16[768,2048]{1,0:T(8,128)(2,1)} copy(bf16[768,2048]{1,0:T(8,128)(2,1)S(1)} %copy-done.2) | data formatting | bytes 6291456
  89.5 1.4 %copy-done.1 = bf16[768,2048]{1,0:T(8,128)(2,1)S(1)} copy-done((bf16[768,2048]{1,0:T(8,128)(2,1)S(1)}, bf16[768,2048]{1,0:T(8,128)(2,1)}, u32[]{:S(2)}) %copy-start.1) | copy-done | bytes 3145752
  90.8 0.0 copy-start
  90.8 1.7 %copy.18 = bf16[768,2048]{1,0:T(8,128)(2,1)} copy(bf16[768,2048]{1,0:T(8,128)(2,1)S(1)} %copy-done.1) | data formatting | bytes 6291456
  92.5 1.4 %copy-done = bf16[768,2048]{1,0:T(8,128)(2,1)S(1)} copy-done((bf16[768,2048]{1,0:T(8,128)(2,1)S(1)}, bf16[768,2048]{1,0:T(8,128)(2,1)}, u32[]{:S(2)}) %copy-start) | copy-done | bytes 3145752
  93.9 0.0 copy-start.3
  93.9 1.7 %copy.19 = bf16[768,2048]{1,0:T(8,128)(2,1)} copy(bf16[768,2048]{1,0:T(8,128)(2,1)S(1)} %copy-done) | data formatting | bytes 6291456
  95.5 0.0 copy-done.3
  95.5 0.6 copy.20
Async XLA Ops:
  83.7 4.1 %copy-start.2 = (bf16[768,2048]{1,0:T(8,128)(2,1)S(1)}, bf16[768,2048]{1,0:T(8,128)(2,1)}, u32[]{:S(2)}) copy-start(bf16[768,2048]{1,0:T(8,128)(2,1)} %get-tuple-element.21) | copy-start | bytes 9437188
  87.8 3.0 %copy-start.1 = (bf16[768,2048]{1,0:T(8,128)(2,1)S(1)}, bf16[768,2048]{1,0:T(8,128)(2,1)}, u32[]{:S(2)}) copy-start(bf16[768,2048]{1,0:T(8,128)(2,1)} %get-tuple-element.22) | copy-start | bytes 9437188
  90.8 3.0 %copy-start = (bf16[768,2048]{1,0:T(8,128)(2,1)S(1)}, bf16[768,2048]{1,0:T(8,128)(2,1)}, u32[]{:S(2)}) copy-start(bf16[768,2048]{1,0:T(8,128)(2,1)} %get-tuple-element.23) | copy-start | bytes 9437188
  93.9 1.7 %copy-start.3 = (f32[16,128]{1,0:T(8,128)S(1)}, f32[16,128]{1,0:T(8,128)}, u32[]{:S(2)}) copy-start(f32[16,128]{1,0:T(8,128)} %get-tuple-element.14) | copy-start | bytes 24580

commit v2 on v1

--- a/solution.py
+++ b/solution.py
@@ -33,17 +33,78 @@
     )
 
 
+def tile(ref, h, j):
+    return ref[j * DH:(j + 1) * DH, pl.ds(pl.multiple_of(h * DH, DH), DH)]
+
+
+def put(ref, h, j, value):
+    ref[j * DH:(j + 1) * DH, pl.ds(pl.multiple_of(h * DH, DH), DH)] = value
+
+
+def inter_grads(sizes, h, to, k, v, cb, sbf, att, gvi, gk, gv):
+    for j in range(sizes[0] // DH):
+        cum = cb[h, j * DH:(j + 1) * DH, :]
+        low = sbf[h, j]
+        tail = jnp.exp(cum[DH - 1:DH, :] - cum)
+        kj, vj = tile(k, h, j), tile(v, h, j)
+        put(gk, to, j, (tile(att, h, j) + tail * nt(vj, low)).astype(BF16))
+        put(gv, to, j, (tile(gvi, h, j) + tail * nn(kj, low)).astype(BF16))
+
+
+def finish(
+    sizes,
+    q, k, v, g, cb, sbf, att, gvi, gg,
+    out_hbm, gq_hbm, gk_hbm, gv_hbm, gg_out,
+    gk, gv, sem, head_sem,
+):
+    HH = sizes[1] // 2
+    HW = HH * DH
+    core = lax.axis_index("seq") % 2
+    own = pl.ds(pl.multiple_of(core * HW, HW), HW)
+    copies = [
+        pltpu.make_async_copy(src, dst, sem.at[n])
+        for n, (src, dst) in enumerate((
+            (g, out_hbm), (q, gq_hbm),
+            (k.at[:, own], gk_hbm.at[:, own]), (v.at[:, own], gv_hbm.at[:, own]),
+        ))
+    ]
+    for c in copies:
+        c.start()
+    gg_out[...] = gg[...]
+
+    def stores(r):
+        src = pl.ds(pl.multiple_of(r * DH, DH), DH)
+        dst = pl.ds(pl.multiple_of(((1 - core) * HH + r) * DH, DH), DH)
+        return [
+            pltpu.make_async_copy(a.at[:, src], b.at[:, dst], head_sem.at[n, r])
+            for n, (a, b) in enumerate(((gk, gk_hbm), (gv, gv_hbm)))
+        ]
+
+    def one(r, carry):
+        inter_grads(sizes, (1 - core) * HH + r, r, k, v, cb, sbf, att, gvi, gk, gv)
+        for c in stores(r):
+            c.start()
+        return carry
+
+    lax.fori_loop(0, HH, one, 0)
+    for r in range(HH):
+        for c in stores(r):
+            c.wait()
+    for c in copies:
+        c.wait()
+
+
 def kernel(
     sizes,
     q_in, k_in, v_in, ld, gain, g_in,
-    out_hbm, gq_hbm, gk_hbm, gv_hbm, gg_out,
-    q, k, v, g, cb, rc, ms, att, gvi, sbf, ga, qt,
+    q, k, v, g, cb, sbf, att, gvi, gg_out,
+    rc, ms, ga,
     acc_s, acc_c, invb, cenb, sums, hx,
     dec_own, dec_par, dec_chip, dec_all,
     loc, lpr, tot, rx, px, pin, st, pst,
     gloc, glpr, gtot, grx, gpx, gpin, gst, gpst,
     ggp, ggpr, ggc, ggrx, ggsum, ggall,
-    in_sem, out_sem, dp_s, dp_r, da_s, da_r, hx_s, hx_r,
+    in_sem, dp_s, dp_r, da_s, da_r, hx_s, hx_r,
     lp_s, lp_r, rx_s, rx_r, pi_s, pi_r, ps_s, ps_r,
     glp_s, glp_r, grx_s, grx_r, gpi_s, gpi_r, gps_s, gps_r,
     gp_s, gp_r, gr_s, gr_r, ga_s, ga_r,
@@ -113,12 +174,6 @@
     dec_copy = remote(dec_own, dec_par, dp_s.at[0], dp_r.at[0], {"seq": mate})
     dec_copy.start()
 
-    def tile(ref, h, j):
-        return ref[j * DH:(j + 1) * DH, pl.ds(pl.multiple_of(h * DH, DH), DH)]
-
-    def put(ref, h, j, value):
-        ref[j * DH:(j + 1) * DH, pl.ds(pl.multiple_of(h * DH, DH), DH)] = value
-
     def cums(h, j):
         return cb[h, j * DH:(j + 1) * DH, :]
 
@@ -215,7 +270,7 @@
             decay = jnp.exp(jnp.where(lower, cums(h, j) - cum_row(h, j), -jnp.inf))
             weights = (nt(qj, tile(k, h, j)) * decay).astype(BF16)
             put(att, h, j, nn(weights, tile(v, h, j)))
-            qt[h, :, j * DH:(j + 1) * DH] = qj.T
+            put(gvi, h, j, qj.astype(F32).T)
 
     loop(HH, intra)
     others(lambda i: remote(dec_chip, dec_all.at[i], da_s.at[i], da_r.at[i], at(i)).wait())
@@ -287,7 +342,7 @@
             center = cenb[j * DH:(j + 1) * DH, :]
             low = (inverse * (grad * scale - normed * center)).astype(BF16)
             put(ga, h, j, low)
-            lifted = qt[h, :, j * DH:(j + 1) * DH].astype(F32) * jnp.exp(cum_row(h, j))
+            lifted = tile(gvi, h, j) * jnp.exp(cum_row(h, j))
             ms[h, j] = nn(lifted.astype(BF16), low)
         ggp[h] = gain_part
         state = ms[h, NJ - 1]
@@ -304,8 +359,6 @@
     loop(HH, lambda r: normalize(own0 + r))
     gain_copy = to_mate(ggp, ggpr, gp_s, gp_r, 0)
     gain_copy.start()
-    store_out = pltpu.make_async_copy(g, out_hbm, out_sem.at[0])
-    store_out.start()
     loop(HH, lambda r: to_mate(gloc.at[oth0 + r], glpr.at[r], glp_s, glp_r, r).wait())
     scan_total(core == 1, gloc, glpr, gtot)
     others(lambda i: out_copy(gtot, grx, grx_s, grx_r, i).start())
@@ -341,38 +394,29 @@
     others(lambda i: remote(ggsum, ggall.at[chip], ga_s.at[i], ga_r.at[chip], at(i)).start())
     ggall[chip] = part
     loop(HH, lambda r: intra_grads(HH + r))
-    store_q = pltpu.make_async_copy(q, gq_hbm, out_sem.at[1])
-    store_q.start()
     others(lambda i: home_copy(gpx, gpin, gpi_s, gpi_r, i).wait_recv())
     settle(core == 1, gpin, gloc, glpr, gst, gpst)
     loop(HH, lambda r: to_mate(gpst.at[r], gst.at[own0 + r], gps_s, gps_r, r).start())
 
-    def inter_grads(h):
+    def later_states(h):
         state = gst[h]
         for j in range(NJ - 1, -1, -1):
-            cum = cums(h, j)
-            end = cum[DH - 1:DH, :]
-            low = state.astype(BF16)
-            tail = jnp.exp(end - cum)
-            kj, vj = tile(k, h, j), tile(v, h, j)
-            gk = tile(att, h, j) + tail * nt(vj, low)
-            gv = tile(gvi, h, j) + tail * nn(kj, low)
-            put(k, h, j, gk.astype(BF16))
-            put(v, h, j, gv.astype(BF16))
+            sbf[h, j] = state.astype(BF16)
             if j > 0:
-                state = jnp.exp(end) * state + ms[h, j]
-
-    loop(HH, lambda r: inter_grads(own0 + r))
-
-    def grads_half(r):
+                state = jnp.exp(cb[h, j * DH + DH - 1:j * DH + DH, :]) * state + ms[h, j]
+
+    def own_grads(r):
+        later_states(own0 + r)
+        inter_grads(sizes, own0 + r, own0 + r, k, v, cb, sbf, att, gvi, k, v)
+
+    loop(HH, own_grads)
+    loop(HH, lambda r: to_mate(gpst.at[r], gst.at[own0 + r], gps_s, gps_r, r).wait_send())
+
+    def mate_states(r):
         to_mate(gpst.at[r], gst.at[oth0 + r], gps_s, gps_r, r).wait_recv()
-        inter_grads(oth0 + r)
-
-    loop(HH, grads_half)
-    store_k = pltpu.make_async_copy(k, gk_hbm, out_sem.at[2])
-    store_k.start()
-    store_v = pltpu.make_async_copy(v, gv_hbm, out_sem.at[3])
-    store_v.start()
+        later_states(oth0 + r)
+
+    loop(HH, mate_states)
     others(lambda i: remote(ggsum, ggall.at[i], ga_s.at[i], ga_r.at[i], at(i)).wait())
     for h in range(H):
         gg_out[h:h + 1, :] = jnp.sum(ggall[h], axis=0, keepdims=True)
@@ -382,9 +426,6 @@
     others(lambda i: in_copy(gtot, grx, grx_s, grx_r, i).wait_send())
     others(lambda i: home_copy(gpx, gpin, gpi_s, gpi_r, i).wait_send())
     loop(HH, lambda r: to_mate(pst.at[r], st.at[oth0 + r], ps_s, ps_r, r).wait_send())
-    loop(HH, lambda r: to_mate(gpst.at[r], gst.at[oth0 + r], gps_s, gps_r, r).wait_send())
-    for c in (store_out, store_q, store_k, store_v):
-        c.wait()
 
 
 def on_device(sizes, queries, key_rows, value_rows, log_decay, norm_gain, grad_out):
@@ -401,32 +442,46 @@
     ]
     scan_sems = [D((HH,)), D((HH,)), D((NC,)), D((NC,)), D((NC,)), D((NC,)), D((HH,)), D((HH,))]
     scratch = [
-        V((T, W), BF16), V((T, W), BF16), V((T, W), BF16), V((T, W), BF16),
-        V((H, T, DH), F32), V((H, 1, T), F32), V((H, NJ, DH, DH), F32), V((T, W), F32),
-        V((T, W), F32), V((H, NJ, DH, DH), BF16), V((T, W), BF16), V((H, DH, T), BF16),
+        V((H, 1, T), F32), V((H, NJ, DH, DH), F32), V((T, W), BF16),
         V((T, DH), F32), V((T, DH), F32), V((T, DH), F32), V((T, DH), F32),
         V((8, T), F32), V((NY, 8, T), F32),
         V((H, 1, DH), F32), V((H, 1, DH), F32), V((H, 1, DH), F32), V((NC, H, 1, DH), F32),
         *mate_scan, *mate_scan,
         V((H, 8, DH), F32), V((H, 8, DH), F32), V((H, 8, DH), F32), V((NC, 8, DH), F32),
         V((8, DH), F32), V((NC, 8, DH), F32),
-        D((4,)), D((4,)), D((1,)), D((1,)), D((NC,)), D((NC,)), D((NY,)), D((NY,)),
+        D((4,)), D((1,)), D((1,)), D((NC,)), D((NC,)), D((NY,)), D((NY,)),
         *scan_sems, *scan_sems,
         D((1,)), D((1,)), D((NC,)), D((NC,)), D((NC,)), D((NC,)),
     ]
-    big = jax.ShapeDtypeStruct((T, W), BF16)
     anywhere = pl.BlockSpec(memory_space=pl.ANY)
-    local = pl.BlockSpec(memory_space=pltpu.VMEM)
-    *grads, gain_grad = pl.pallas_call(
+    local = pl.BlockSpec(memory_space=V)
+    held = (
+        V((T, W), BF16), V((T, W), BF16), V((T, W), BF16), V((T, W), BF16),
+        V((H, T, DH), F32), V((H, NJ, DH, DH), BF16), V((T, W), F32), V((T, W), F32),
+        V((H, DH), F32),
+    )
+    parts = pl.pallas_call(
         functools.partial(kernel, sizes),
-        out_shape=(big, big, big, big, jax.ShapeDtypeStruct((H, DH), F32)),
+        out_shape=held,
         in_specs=[anywhere, anywhere, anywhere, local, local, anywhere],
-        out_specs=(anywhere, anywhere, anywhere, anywhere, local),
+        out_specs=(local,) * len(held),
         scratch_shapes=scratch,
         compiler_params=pltpu.CompilerParams(
-            collective_id=0, has_side_effects=True, vmem_limit_bytes=66_000_000
+            collective_id=0, has_side_effects=True, vmem_limit_bytes=24 << 20
         ),
     )(queries, key_rows, value_rows, log_decay, norm_gain.reshape(1, W), grad_out)
+    parts = [pltpu.with_memory_space_constraint(x, V) for x in parts]
+    big = jax.ShapeDtypeStruct((T, W), BF16)
+    *grads, gain_grad = pl.pallas_call(
+        functools.partial(finish, sizes),
+        out_shape=(big, big, big, big, jax.ShapeDtypeStruct((H, DH), F32)),
+        in_specs=[local] * len(held),
+        out_specs=(anywhere, anywhere, anywhere, anywhere, local),
+        scratch_shapes=[
+            V((T, W // 2), BF16), V((T, W // 2), BF16), D((4,)), D((2, HH)),
+        ],
+        compiler_params=pltpu.CompilerParams(vmem_limit_bytes=5 << 20),
+    )(*parts)
     return (*grads, gain_grad.reshape(W))
 
 

time: 96.4 us -> 85 us (0.88)
  local copies, waits for them, and re-layouts: 12.4 us -> 0 us
  Pallas kernels: 83 us -> 84.2 us
    unnamed x13 -> x0, local copies, waits for them, and re-layouts: 12.4 us -> none
    pallas_call x1 -> x2, Pallas kernels: 83 us -> 84.2 us  [the longest x1 78.9 us: on_device(): pl.pallas_call(functools.partial(kernel, sizes), out_shape=held, in_specs...]
where the time goes in v2:
time: 85 us; the launch traced here: 84.9 us
  Pallas kernels  84.2 us (99%)
    pallas_call x1, Pallas kernels, on_device(): pl.pallas_call(functools.partial(kernel, sizes), out_shape=held, in_specs...  78.9 us
    pallas_call x1, Pallas kernels, on_device(): pl.pallas_call(functools.partial(finish, sizes), out_shape=(big, big, big...  5.36 us

profile of v2, /device:TPU:1, one launch (start us, length us, event | category | flops | bytes accessed | tf_op | source)
XLA Modules:
  0.0 84.9 jit_solution(13858987651046570001)
XLA Ops:
  0.6 78.9 %shard_map.101 = (bf16[768,2048]{1,0:T(8,128)(2,1)S(1)}, bf16[768,2048]{1,0:T(8,128)(2,1)S(1)}, bf16[768,2048]{1,0:T(8,128)(2,1)S(1)}, bf16[768,2048]{1,0:T(8,12...) custom-call(bf16[768,2048]{1,0:T(8,128)(2,1)} %q_in.1, ...), custom_call_target="tpu_custom_call" | custom-call | tf_op jit(solution)/shard_map/pallas_call | solution.py:463
  79.5 5.4 %shard_map.102 = (bf16[768,2048]{1,0:T(8,128)(2,1)}, bf16[768,2048]{1,0:T(8,128)(2,1)}, bf16[768,2048]{1,0:T(8,128)(2,1)}, bf16[768,2048]{1,0:T(8,128)(2,1)}, f32[16,128]{1,0:T(8,128)}) custom-call(bf16[768,2048]{1,0:T(8,128)(2,1)S(1)} %get-tuple-element.19.q, bf16[768,2048]{1,0:T(8,128)(2,1)S(1)} %get-tuple-element.20.k, ...), custom_call_target="tpu_custom_call" | custom-call | tf_op jit(solution)/shard_map/pallas_call | solution.py:475

commit v3 on v2

v3 whole, which is shorter than its diff:
```python
import functools

import jax
import jax.numpy as jnp
from jax import lax
from jax.experimental import pallas as pl
from jax.experimental.pallas import tpu as pltpu
from jax.sharding import PartitionSpec as P

DH = 128
EPSILON = 1e-06
F32 = jnp.float32
BF16 = jnp.bfloat16
MESH = pl.DeviceIdType.MESH
HIGHEST = lax.Precision.HIGHEST


def nn(a, b):
    return lax.dot_general(a, b, (((1,), (0,)), ((), ())), preferred_element_type=F32)


def nt(a, b):
    return lax.dot_general(a, b, (((1,), (1,)), ((), ())), preferred_element_type=F32)


def tn(a, b):
    return lax.dot_general(a, b, (((0,), (0,)), ((), ())), preferred_element_type=F32)


def exact_nt(a, b):
    return lax.dot_general(
        a, b, (((1,), (1,)), ((), ())), preferred_element_type=F32, precision=HIGHEST
    )


def tile(ref, h, j):
    return ref[j * DH:(j + 1) * DH, pl.ds(pl.multiple_of(h * DH, DH), DH)]


def put(ref, h, j, value):
    ref[j * DH:(j + 1) * DH, pl.ds(pl.multiple_of(h * DH, DH), DH)] = value


def inter_grads(sizes, h, to, k, v, cb, sbf, att, gvi, gk, gv):
    for j in range(sizes[0] // DH):
        cum = cb[h, j * DH:(j + 1) * DH, :]
        low = sbf[h, j]
        tail = jnp.exp(cum[DH - 1:DH, :] - cum)
        kj, vj = tile(k, h, j), tile(v, h, j)
        put(gk, to, j, (tile(att, h, j) + tail * nt(vj, low)).astype(BF16))
        put(gv, to, j, (tile(gvi, h, j) + tail * nn(kj, low)).astype(BF16))


def finish(
    sizes,
    q, k, v, g, cb, sbf, att, gvi, gg,
    out_hbm, gq_hbm, gk_hbm, gv_hbm, gg_out,
    gk, gv, sem, head_sem,
):
    HH = sizes[1] // 2
    HW = HH * DH
    core = lax.axis_index("seq") % 2
    own = pl.ds(pl.multiple_of(core * HW, HW), HW)
    copies = [
        pltpu.make_async_copy(src, dst, sem.at[n])
        for n, (src, dst) in enumerate((
            (g, out_hbm), (q, gq_hbm),
            (k.at[:, own], gk_hbm.at[:, own]), (v.at[:, own], gv_hbm.at[:, own]),
        ))
    ]
    for c in copies:
        c.start()
    gg_out[...] = gg[...]

    def stores(r):
        src = pl.ds(pl.multiple_of(r * DH, DH), DH)
        dst = pl.ds(pl.multiple_of(((1 - core) * HH + r) * DH, DH), DH)
        return [
            pltpu.make_async_copy(a.at[:, src], b.at[:, dst], head_sem.at[n, r])
            for n, (a, b) in enumerate(((gk, gk_hbm), (gv, gv_hbm)))
        ]

    def one(r, carry):
        inter_grads(sizes, (1 - core) * HH + r, r, k, v, cb, sbf, att, gvi, gk, gv)
        for c in stores(r):
            c.start()
        return carry

    lax.fori_loop(0, HH, one, 0)
    for r in range(HH):
        for c in stores(r):
            c.wait()
    for c in copies:
        c.wait()


def kernel(
    sizes,
    q_in, k_in, v_in, ld, gain, g_in,
    q, k, v, g, cb, sbf, att, gvi, gg_out,
    rc, ms, ga, kt, wt,
    acc_s, acc_c, sums, hx,
    dec_own, dec_par, dec_chip, dec_all,
    loc, tot, px, pst, lpr, rx, pin, st,
    ggp, ggpr, ggc, ggrx, ggsum, ggall,
    in_sem, dp_s, dp_r, da_s, da_r, hx_s, hx_r,
    lp_s, lp_r, rx_s, rx_r, pi_s, pi_r, ps_s, ps_r,
    glp_s, glp_r, grx_s, grx_r, gpi_s, gpi_r, gps_s, gps_r,
    gp_s, gp_r, gr_s, gr_r, ga_s, ga_r,
):
    T, H, NC, NY = sizes
    NJ = T // DH
    HH = H // 2
    HG = HH // 2
    RS = HG * DH // NC
    HD = NY * H * DH
    PAIR = 2 if HG % 2 == 0 else 1
    me = lax.axis_index("seq")
    y = lax.axis_index("head")
    chip = me // 2
    core = me % 2
    mate = {"seq": chip * 2 + (1 - core)}
    own0 = core * HH
    oth0 = (1 - core) * HH

    def at(i):
        return {"seq": i * 2 + core}

    def remote(src, dst, s, r, dev):
        return pltpu.make_async_remote_copy(
            src_ref=src, dst_ref=dst, send_sem=s, recv_sem=r, device_id=dev, device_id_type=MESH
        )

    def loop(n, body):
        lax.fori_loop(0, n, lambda i, c: (body(i), c)[1], 0)

    def others(body):
        lax.fori_loop(1, NC, lambda r, c: (body(lax.rem(chip + r, NC)), c)[1], 0)

    loads = [
        pltpu.make_async_copy(src, dst, in_sem.at[n])
        for n, (src, dst) in enumerate(((k_in, k), (v_in, v), (q_in, q), (g_in, g)))
    ]
    loads[0].start()
    loads[1].start()

    barrier = pltpu.get_barrier_semaphore()
    others(
        lambda i: pl.semaphore_signal(barrier, inc=1, device_id=at(i), device_id_type=MESH)
    )
    pl.semaphore_signal(barrier, inc=1, device_id=mate, device_id_type=MESH)
    for r in range(1, NY):
        pl.semaphore_signal(
            barrier, inc=1, device_id={"head": lax.rem(y + r, NY)}, device_id_type=MESH
        )

    row_i = lax.broadcasted_iota(jnp.int32, (DH, DH), 0)
    col_i = lax.broadcasted_iota(jnp.int32, (DH, DH), 1)
    lower = row_i >= col_i
    tri = jnp.where(lower, 1.0, 0.0).astype(F32)

    total = jnp.zeros((H, 1), F32)
    for j in range(NJ):
        piece = ld[:, j * DH:(j + 1) * DH]
        rows = exact_nt(piece, tri)
        columns = exact_nt(tri, piece)
        for h in range(H):
            rc[h, :, j * DH:(j + 1) * DH] = rows[h:h + 1, :]
            cb[h, j * DH:(j + 1) * DH, :] = jnp.broadcast_to(columns[:, h:h + 1], (DH, DH))
        total = total + rows[:, DH - 1:DH]
    dec_own[...] = jnp.broadcast_to(total, (H, DH)).reshape(H, 1, DH)
    loads[2].start()
    loads[3].start()

    def cums(h, j):
        return cb[h, j * DH:(j + 1) * DH, :]

    def cum_row(h, j):
        return rc[h, :, j * DH:(j + 1) * DH]

    def local_states(h):
        state = None
        for j in range(NJ):
            row = cum_row(h, j)
            end = row[:, DH - 1:DH]
            flipped = tile(k, h, j).T
            put(kt, h, j, flipped)
            scaled = (flipped.astype(F32) * jnp.exp(end - row)).astype(BF16)
            part = nn(scaled, tile(v, h, j))
            ms[h, j] = part
            last = jnp.exp(cb[h, j * DH + DH - 1:j * DH + DH, :])
            state = part if state is None else last * state + part
        loc[h] = state

    def group(ref, base, n):
        return ref.at[pl.ds(base + n * HG, HG)]

    def swap(src, recv, s, r, n):
        return remote(group(src, oth0, n), recv.at[n], s.at[n], r.at[n], mate)

    def give(dst, s, r, n, base):
        return remote(pst.at[n], group(dst, base, n), s.at[n], r.at[n], mate)

    def scan_total(first, recv, n):
        def one(r):
            h = own0 + n * HG + r
            mine = jnp.where(first, jnp.exp(dec_par[h]), 1.0)
            theirs = jnp.where(first, 1.0, jnp.exp(dec_own[h]))
            tot[n, pl.ds(pl.multiple_of(r * DH, DH), DH), :] = mine * loc[h] + theirs * recv[n, r]

        loop(HG, one)

    def piece_of(ref, n, i):
        return ref.at[n, pl.ds(pl.multiple_of(i * RS, RS), RS), :]

    def send_out(recv, s, r, n):
        others(
            lambda i: remote(piece_of(tot, n, i), recv.at[n, chip], s.at[n], r.at[n], at(i)).start()
        )

    def all_out(recv, s, r, n):
        return remote(
            tot.at[n, pl.ds(0, (NC - 1) * RS), :], tot.at[n, pl.ds(0, (NC - 1) * RS), :],
            s.at[n], r.at[n], mate,
        )

    def all_in(recv, s, r, n):
        part = recv.at[n, pl.ds(0, NC - 1)]
        return remote(part, part, s.at[n], r.at[n], mate)

    def send_back(dst, s, r, n):
        others(
            lambda i: remote(px.at[n, i], piece_of(dst, n, chip), s.at[n], r.at[n], at(i)).start()
        )

    def all_back(s, r, n):
        part = px.at[n, pl.ds(0, NC - 1)]
        return remote(part, part, s.at[n], r.at[n], mate)

    def all_home(dst, s, r, n):
        part = dst.at[n, pl.ds(0, (NC - 1) * RS), :]
        return remote(part, part, s.at[n], r.at[n], mate)

    def prefix(recv, dst, s, r, n, reverse):
        head = own0 + n * HG + (chip * RS) // DH
        mine = pl.ds(pl.multiple_of(chip * RS, RS), RS)
        recv[n, chip] = tot[n, mine, :]
        all_in(recv, s, r, n).wait_recv()
        state = jnp.zeros((RS, DH), F32)
        for i in reversed(range(NC)) if reverse else range(NC):
            px[n, i] = state
            state = jnp.exp(dec_all[i, head]) * state + recv[n, i]
        dst[n, mine, :] = px[n, chip]

    def settle(first, homed, recv, dst, n):
        def one(r):
            h = own0 + n * HG + r
            state = homed[n, pl.ds(pl.multiple_of(r * DH, DH), DH), :]
            ahead = jnp.where(first, 1.0, jnp.exp(dec_par[h]))
            dst[h] = ahead * state + jnp.where(first, 0.0, recv[n, r])
            after = jnp.where(first, jnp.exp(dec_own[h]), 1.0)
            pst[n, r] = after * state + jnp.where(first, loc[h], 0.0)

        loop(HG, one)

    dec_copy = remote(dec_own, dec_par, dp_s.at[0], dp_r.at[0], mate)

    def dec_send(i):
        return remote(dec_chip, dec_all.at[chip], da_s.at[0], da_r.at[0], at(i))

    dec_part = dec_all.at[pl.ds(0, NC - 1)]
    dec_done = remote(dec_part, dec_part, da_s.at[0], da_r.at[0], mate)

    loads[0].wait()
    loads[1].wait()
    loop(HG, lambda r: local_states(oth0 + r))
    pl.semaphore_wait(barrier, NC - 1 + 1 + NY - 1)
    dec_copy.start()
    swap(loc, lpr, lp_s, lp_r, 0).start()
    loop(HG, lambda r: local_states(own0 + r))
    dec_copy.wait()
    dec_chip[...] = dec_own[...] + dec_par[...]
    dec_all[chip] = dec_chip[...]
    others(lambda i: dec_send(i).start())
    swap(loc, lpr, lp_s, lp_r, 0).wait()
    scan_total(core == 0, lpr, 0)
    loop(HG, lambda r: local_states(oth0 + HG + r))
    send_out(rx, rx_s, rx_r, 0)
    swap(loc, lpr, lp_s, lp_r, 1).start()
    loop(HG, lambda r: local_states(own0 + HG + r))
    swap(loc, lpr, lp_s, lp_r, 1).wait()
    scan_total(core == 0, lpr, 1)
    send_out(rx, rx_s, rx_r, 1)

    loads[2].wait()

    def intra(h):
        for j in range(NJ):
            qj, vj = tile(q, h, j), tile(v, h, j)
            decay = jnp.exp(jnp.where(lower, cums(h, j) - cum_row(h, j), -jnp.inf))
            weights = (nn(qj, tile(kt, h, j)) * decay).astype(BF16)
            put(att, h, j, nn(weights, vj))
            put(wt, h, j, weights.T)
            put(ga, h, j, qj.T)
            put(kt, h, j, vj.T)

    def spans(n):
        first = (3 * n) // 8
        second = (6 * n) // 8
        return first, second

    cut0, cut1 = spans(H)
    loop(cut0, intra)
    dec_done.wait()
    prefix(rx, pin, rx_s, rx_r, 0, False)
    send_back(pin, pi_s, pi_r, 0)
    loop(cut1 - cut0, lambda r: intra(cut0 + r))
    prefix(rx, pin, rx_s, rx_r, 1, False)
    send_back(pin, pi_s, pi_r, 1)
    loop(H - cut1, lambda r: intra(cut1 + r))
    loads[3].wait()
    acc_s[...] = jnp.zeros_like(acc_s)
    acc_c[...] = jnp.zeros_like(acc_c)

    def inter(h):
        states = [st[h + p] for p in range(PAIR)]
        scales = [gain[:, pl.ds(pl.multiple_of((h + p) * DH, DH), DH)] for p in range(PAIR)]
        for j in range(NJ):
            squares, crosses = None, None
            for p in range(PAIR):
                cum = cums(h + p, j)
                low = states[p].astype(BF16)
                sbf[h + p, j] = low
                mixed = tile(att, h + p, j) + jnp.exp(cum) * nn(tile(q, h + p, j), low)
                put(att, h + p, j, mixed)
                square = mixed * mixed
                cross = tile(g, h + p, j).astype(F32) * scales[p] * mixed
                squares = square if squares is None else squares + square
                crosses = cross if crosses is None else crosses + cross
                if j < NJ - 1:
                    states[p] = jnp.exp(cum[DH - 1:DH, :]) * states[p] + ms[h + p, j]
            acc_s[j * DH:(j + 1) * DH, :] += squares
            acc_c[j * DH:(j + 1) * DH, :] += crosses

    for n in range(2):
        all_home(pin, pi_s, pi_r, n).wait_recv()
        settle(core == 0, pin, lpr, st, n)
        give(st, ps_s, ps_r, n, own0).start()
        loop(HG // PAIR, lambda r: inter(own0 + n * HG + r * PAIR))
    for n in range(2):
        give(st, ps_s, ps_r, n, oth0).wait_recv()
        loop(HG // PAIR, lambda r: inter(oth0 + n * HG + r * PAIR))

    pick = lax.broadcasted_iota(jnp.int32, (8, DH), 0) == 0
    for j in range(NJ):
        a = jnp.sum(acc_s[j * DH:(j + 1) * DH, :].T, axis=0, keepdims=True)
        b = jnp.sum(acc_c[j * DH:(j + 1) * DH, :].T, axis=0, keepdims=True)
        sums[:, j * DH:(j + 1) * DH] = jnp.where(pick, a, b)
    for r in range(1, NY):
        d = lax.rem(y + r, NY)
        remote(sums, hx.at[y], hx_s.at[0], hx_r.at[0], {"head": d}).start()
    hx[y] = sums[...]

    def turn(h):
        for j in range(NJ):
            sbf[h, j] = sbf[h, j].T

    loop(H, turn)
    for n in range(2):
        all_out(rx, rx_s, rx_r, n).wait_send()
        all_back(pi_s, pi_r, n).wait_send()
        give(st, ps_s, ps_r, n, own0).wait_send()
    hx_part = hx.at[pl.ds(0, NY - 1)]
    remote(hx_part, hx_part, hx_s.at[0], hx_r.at[0], mate).wait()
    for j in range(NJ):
        both = hx[0, :, j * DH:(j + 1) * DH]
        for r in range(1, NY):
            both = both + hx[r, :, j * DH:(j + 1) * DH]
        inverse = lax.rsqrt(both[0:1, :] / HD + EPSILON)
        center = both[1:2, :] * inverse / HD
        columns = jnp.where(pick, inverse, center).T
        acc_s[j * DH:(j + 1) * DH, :] = jnp.broadcast_to(columns[:, 0:1], (DH, DH))
        acc_c[j * DH:(j + 1) * DH, :] = jnp.broadcast_to(columns[:, 1:2], (DH, DH))

    def normalize(h):
        scale = gain[:, pl.ds(pl.multiple_of(h * DH, DH), DH)]
        gain_part = jnp.zeros((8, DH), F32)
        for j in range(NJ):
            inverse = acc_s[j * DH:(j + 1) * DH, :]
            normed = tile(att, h, j) * inverse
            grad = tile(g, h, j).astype(F32)
            put(g, h, j, (normed * scale).astype(BF16))
            gain_part = gain_part + jnp.sum((grad * normed).reshape(DH // 8, 8, DH), axis=0)
            center = acc_c[j * DH:(j + 1) * DH, :]
            low = (inverse * (grad * scale - normed * center)).astype(BF16)
            lifted = tile(ga, h, j).astype(F32) * jnp.exp(cum_row(h, j))
            ms[h, j] = nn(lifted.astype(BF16), low)
            put(ga, h, j, low)
        ggp[h] = gain_part
        state = ms[h, NJ - 1]
        for j in range(NJ - 2, -1, -1):
            end = cb[h, j * DH + DH - 1:j * DH + DH, :]
            state = jnp.exp(end) * state + ms[h, j]
        loc[h] = state

    for n in range(2):
        loop(HG, lambda r: normalize(oth0 + n * HG + r))
        swap(loc, lpr, glp_s, glp_r, n).start()
        loop(HG, lambda r: normalize(own0 + n * HG + r))
        swap(loc, lpr, glp_s, glp_r, n).wait()
        scan_total(core == 1, lpr, n)
        send_out(rx, grx_s, grx_r, n)

    gain_copy = remote(ggp, ggpr, gp_s.at[0], gp_r.at[0], mate)
    gain_copy.start()

    def intra_grads(h):
        for j in range(NJ):
            gj = tile(ga, h, j)
            cum = cums(h, j)
            decay = jnp.exp(jnp.where(lower, cum - cum_row(h, j), -jnp.inf))
            gw = (nn(gj, tile(kt, h, j)) * decay).astype(BF16)
            gq = nn(gw, tile(k, h, j)) + jnp.exp(cum) * nn(gj, sbf[h, j])
            put(gvi, h, j, nn(tile(wt, h, j), gj))
            put(att, h, j, nn(gw.T, tile(q, h, j)))
            put(q, h, j, gq.astype(BF16))

    loop(cut0, intra_grads)
    gain_copy.wait()
    ggc[...] = ggp[...] + ggpr[...]
    ggrx[chip] = ggc[chip]
    prefix(rx, pin, grx_s, grx_r, 0, True)
    send_back(pin, gpi_s, gpi_r, 0)
    others(lambda i: remote(ggc.at[i], ggrx.at[chip], gr_s.at[0], gr_r.at[0], at(i)).start())
    loop(cut1 - cut0, lambda r: intra_grads(cut0 + r))
    prefix(rx, pin, grx_s, grx_r, 1, True)
    send_back(pin, gpi_s, gpi_r, 1)
    gr_part = ggrx.at[pl.ds(0, NC - 1)]
    remote(gr_part, gr_part, gr_s.at[0], gr_r.at[0], mate).wait()
    part = ggrx[0]
    for i in range(1, NC):
        part = part + ggrx[i]
    ggsum[...] = part
    ggall[chip] = part
    others(lambda i: remote(ggsum, ggall.at[chip], ga_s.at[0], ga_r.at[0], at(i)).start())
    loop(H - cut1, lambda r: intra_grads(cut1 + r))

    def later_states(h):
        state = st[h]
        for j in range(NJ - 1, -1, -1):
            sbf[h, j] = state.astype(BF16)
            if j > 0:
                state = jnp.exp(cb[h, j * DH + DH - 1:j * DH + DH, :]) * state + ms[h, j]

    def own_grads(h):
        later_states(h)
        inter_grads(sizes, h, h, k, v, cb, sbf, att, gvi, k, v)

    for n in range(2):
        all_home(pin, gpi_s, gpi_r, n).wait_recv()
        settle(core == 1, pin, lpr, st, n)
        give(st, gps_s, gps_r, n, own0).start()
        loop(HG, lambda r: own_grads(own0 + n * HG + r))
    for n in range(2):
        give(st, gps_s, gps_r, n, oth0).wait_recv()
        loop(HG, lambda r: later_states(oth0 + n * HG + r))

    gg_part = ggall.at[pl.ds(0, NC - 1)]
    remote(gg_part, gg_part, ga_s.at[0], ga_r.at[0], mate).wait()
    for h in range(H):
        gg_out[h:h + 1, :] = jnp.sum(ggall[h], axis=0, keepdims=True)
    for n in range(2):
        all_out(rx, grx_s, grx_r, n).wait_send()
        all_back(gpi_s, gpi_r, n).wait_send()
        give(st, gps_s, gps_r, n, own0).wait_send()


def on_device(sizes, queries, key_rows, value_rows, log_decay, norm_gain, grad_out):
    T, H, NC, NY = sizes
    W = H * DH
    NJ = T // DH
    HH = H // 2
    HG = HH // 2
    RS = HG * DH // NC
    V = pltpu.VMEM
    D = pltpu.SemaphoreType.DMA
    rows = V((2, HG * DH, DH), F32)
    slots = V((2, NC, RS, DH), F32)
    heads = V((2, HG, DH, DH), F32)
    states = V((H, DH, DH), F32)
    scratch = [
        V((H, 1, T), F32), V((H, NJ, DH, DH), F32), V((T, W), BF16), V((T, W), BF16),
        V((T, W), BF16),
        V((T, DH), F32), V((T, DH), F32),
        V((8, T), F32), V((NY, 8, T), F32),
        V((H, 1, DH), F32), V((H, 1, DH), F32), V((H, 1, DH), F32), V((NC, H, 1, DH), F32),
        states, rows, slots, heads, heads, slots, rows, states,
        V((H, 8, DH), F32), V((H, 8, DH), F32), V((H, 8, DH), F32), V((NC, 8, DH), F32),
        V((8, DH), F32), V((NC, 8, DH), F32),
        D((4,)), *[D((1,))] * 6, *[D((2,))] * 16, *[D((1,))] * 6,
    ]
    anywhere = pl.BlockSpec(memory_space=pl.ANY)
    local = pl.BlockSpec(memory_space=V)
    held = (
        V((T, W), BF16), V((T, W), BF16), V((T, W), BF16), V((T, W), BF16),
        V((H, T, DH), F32), V((H, NJ, DH, DH), BF16), V((T, W), F32), V((T, W), F32),
        V((H, DH), F32),
    )
    parts = pl.pallas_call(
        functools.partial(kernel, sizes),
        out_shape=held,
        in_specs=[anywhere, anywhere, anywhere, local, local, anywhere],
        out_specs=(local,) * len(held),
        scratch_shapes=scratch,
        compiler_params=pltpu.CompilerParams(
            collective_id=0, has_side_effects=True, vmem_limit_bytes=23 << 20
        ),
    )(queries, key_rows, value_rows, log_decay, norm_gain.reshape(1, W), grad_out)
    parts = [pltpu.with_memory_space_constraint(x, V) for x in parts]
    big = jax.ShapeDtypeStruct((T, W), BF16)
    *grads, gain_grad = pl.pallas_call(
        functools.partial(finish, sizes),
        out_shape=(big, big, big, big, jax.ShapeDtypeStruct((H, DH), F32)),
        in_specs=[local] * len(held),
        out_specs=(anywhere, anywhere, anywhere, anywhere, local),
        scratch_shapes=[
            V((T, W // 2), BF16), V((T, W // 2), BF16), D((4,)), D((2, HH)),
        ],
        compiler_params=pltpu.CompilerParams(vmem_limit_bytes=5 << 20),
    )(*parts)
    return (*grads, gain_grad.reshape(W))


def solution(mesh):
    def whole(queries, key_rows, value_rows, log_decay, norm_gain, grad_out):
        seq, head = mesh.shape["seq"], mesh.shape["head"]
        sizes = (queries.shape[0] // seq, queries.shape[1] // DH // head, seq // 2, head)
        rows = P("seq", "head")
        return jax.shard_map(
            functools.partial(on_device, sizes),
            mesh=mesh,
            in_specs=(rows, rows, rows, P("head", "seq"), P("head"), rows),
            out_specs=(rows, rows, rows, rows, P("head")),
            check_vma=False,
        )(queries, key_rows, value_rows, log_decay, norm_gain, grad_out)

    return whole
```

time: 85 us -> 71.2 us (0.84)
  Pallas kernels: 84.2 us -> 70.4 us
    pallas_call x1, Pallas kernels: 78.9 us -> 65 us  [on_device(): pl.pallas_call(functools.partial(kernel, sizes), out_shape=held, in_specs...]
where the time goes in v3:
time: 71.2 us; the launch traced here: 71 us
  Pallas kernels  70.4 us (99%)
    pallas_call x1, Pallas kernels, on_device(): pl.pallas_call(functools.partial(kernel, sizes), out_shape=held, in_specs...  65 us
    pallas_call x1, Pallas kernels, on_device(): pl.pallas_call(functools.partial(finish, sizes), out_shape=(big, big, big...  5.36 us

profile of v3, /device:TPU:1, one launch (start us, length us, event | category | flops | bytes accessed | tf_op | source)
XLA Modules:
  0.0 71.0 jit_solution(3168586565604606158)
XLA Ops:
  0.6 65.0 %shard_map.101 = (bf16[768,2048]{1,0:T(8,128)(2,1)S(1)}, bf16[768,2048]{1,0:T(8,128)(2,1)S(1)}, bf16[768,2048]{1,0:T(8,128)(2,1)S(1)}, bf16[768,2048]{1,0:T(8,12...) custom-call(bf16[768,2048]{1,0:T(8,128)(2,1)} %q_in.1, ...), custom_call_target="tpu_custom_call" | custom-call | tf_op jit(solution)/shard_map/pallas_call | solution.py:509
  65.7 5.4 %shard_map.102 = (bf16[768,2048]{1,0:T(8,128)(2,1)}, bf16[768,2048]{1,0:T(8,128)(2,1)}, bf16[768,2048]{1,0:T(8,128)(2,1)}, bf16[768,2048]{1,0:T(8,128)(2,1)}, f32[16,128]{1,0:T(8,128)}) custom-call(bf16[768,2048]{1,0:T(8,128)(2,1)S(1)} %get-tuple-element.19.q, bf16[768,2048]{1,0:T(8,128)(2,1)S(1)} %get-tuple-element.20.k, ...), custom_call_target="tpu_custom_call" | custom-call | tf_op jit(solution)/shard_map/pallas_call | solution.py:521

commit v4 on v3

--- a/solution.py
+++ b/solution.py
@@ -15,6 +15,10 @@
 HIGHEST = lax.Precision.HIGHEST
 
 
+def groups_of(heads):
+    return 4 if heads % 8 == 0 else 2
+
+
 def nn(a, b):
     return lax.dot_general(a, b, (((1,), (0,)), ((), ())), preferred_element_type=F32)
 
@@ -47,7 +51,7 @@
         low = sbf[h, j]
         tail = jnp.exp(cum[DH - 1:DH, :] - cum)
         kj, vj = tile(k, h, j), tile(v, h, j)
-        put(gk, to, j, (tile(att, h, j) + tail * nt(vj, low)).astype(BF16))
+        put(gk, to, j, (tile(att, h, j) + tail * nn(vj, low.T)).astype(BF16))
         put(gv, to, j, (tile(gvi, h, j) + tail * nn(kj, low)).astype(BF16))
 
 
@@ -111,10 +115,12 @@
     T, H, NC, NY = sizes
     NJ = T // DH
     HH = H // 2
-    HG = HH // 2
+    G = groups_of(HH)
+    HG = HH // G
     RS = HG * DH // NC
     HD = NY * H * DH
     PAIR = 2 if HG % 2 == 0 else 1
+    U = H // PAIR
     me = lax.axis_index("seq")
     y = lax.axis_index("head")
     chip = me // 2
@@ -133,6 +139,23 @@
 
     def loop(n, body):
         lax.fori_loop(0, n, lambda i, c: (body(i), c)[1], 0)
+
+    def span(first, n, body):
+        lax.fori_loop(first, n, lambda i, c: (body(i), c)[1], 0)
+
+    def heads(base, body):
+        def one(r):
+            for p in range(PAIR):
+                body(base + r * PAIR + p)
+
+        loop(HG // PAIR, one)
+
+    def units(first, n, body):
+        def one(r):
+            for p in range(PAIR):
+                body((first + r) * PAIR + p)
+
+        loop(n, one)
 
     def others(body):
         lax.fori_loop(1, NC, lambda r, c: (body(lax.rem(chip + r, NC)), c)[1], 0)
@@ -210,11 +233,19 @@
 
         loop(HG, one)
 
+    side = 4 if NC == 16 else 2
+    steps = [(a, b) for a in range(side) for b in range(side) if a + b > 0]
+    steps.sort(key=lambda ab: -sum(min(d, side - d) for d in ab))
+
+    def farthest(body):
+        for a, b in steps:
+            body(lax.rem(chip // side + a, side) * side + lax.rem(chip % side + b, side))
+
     def piece_of(ref, n, i):
         return ref.at[n, pl.ds(pl.multiple_of(i * RS, RS), RS), :]
 
     def send_out(recv, s, r, n):
-        others(
+        farthest(
             lambda i: remote(piece_of(tot, n, i), recv.at[n, chip], s.at[n], r.at[n], at(i)).start()
         )
 
@@ -229,7 +260,7 @@
         return remote(part, part, s.at[n], r.at[n], mate)
 
     def send_back(dst, s, r, n):
-        others(
+        farthest(
             lambda i: remote(px.at[n, i], piece_of(dst, n, chip), s.at[n], r.at[n], at(i)).start()
         )
 
@@ -273,24 +304,28 @@
 
     loads[0].wait()
     loads[1].wait()
-    loop(HG, lambda r: local_states(oth0 + r))
+    heads(oth0, local_states)
     pl.semaphore_wait(barrier, NC - 1 + 1 + NY - 1)
     dec_copy.start()
     swap(loc, lpr, lp_s, lp_r, 0).start()
-    loop(HG, lambda r: local_states(own0 + r))
+
+    def for_mate(n):
+        heads(oth0 + n * HG, local_states)
+        swap(loc, lpr, lp_s, lp_r, n).start()
+
+    span(1, G, for_mate)
     dec_copy.wait()
     dec_chip[...] = dec_own[...] + dec_par[...]
     dec_all[chip] = dec_chip[...]
     others(lambda i: dec_send(i).start())
-    swap(loc, lpr, lp_s, lp_r, 0).wait()
-    scan_total(core == 0, lpr, 0)
-    loop(HG, lambda r: local_states(oth0 + HG + r))
-    send_out(rx, rx_s, rx_r, 0)
-    swap(loc, lpr, lp_s, lp_r, 1).start()
-    loop(HG, lambda r: local_states(own0 + HG + r))
-    swap(loc, lpr, lp_s, lp_r, 1).wait()
-    scan_total(core == 0, lpr, 1)
-    send_out(rx, rx_s, rx_r, 1)
+
+    def for_own(n):
+        heads(own0 + n * HG, local_states)
+        swap(loc, lpr, lp_s, lp_r, n).wait()
+        scan_total(core == 0, lpr, n)
+        send_out(rx, rx_s, rx_r, n)
+
+    loop(G, for_own)
 
     loads[2].wait()
 
@@ -301,23 +336,21 @@
             weights = (nn(qj, tile(kt, h, j)) * decay).astype(BF16)
             put(att, h, j, nn(weights, vj))
             put(wt, h, j, weights.T)
-            put(ga, h, j, qj.T)
+            lifted = qj.T.astype(F32) * jnp.exp(cum_row(h, j))
+            put(ga, h, j, lifted.astype(BF16))
             put(kt, h, j, vj.T)
 
-    def spans(n):
-        first = (3 * n) // 8
-        second = (6 * n) // 8
-        return first, second
-
-    cut0, cut1 = spans(H)
-    loop(cut0, intra)
+    ahead = U // 4
+    units(0, ahead, intra)
     dec_done.wait()
-    prefix(rx, pin, rx_s, rx_r, 0, False)
-    send_back(pin, pi_s, pi_r, 0)
-    loop(cut1 - cut0, lambda r: intra(cut0 + r))
-    prefix(rx, pin, rx_s, rx_r, 1, False)
-    send_back(pin, pi_s, pi_r, 1)
-    loop(H - cut1, lambda r: intra(cut1 + r))
+
+    def forward(n):
+        prefix(rx, pin, rx_s, rx_r, n, False)
+        send_back(pin, pi_s, pi_r, n)
+        units(ahead + n, 1, intra)
+
+    loop(G, forward)
+    units(ahead + G, U - ahead - G, intra)
     loads[3].wait()
     acc_s[...] = jnp.zeros_like(acc_s)
     acc_c[...] = jnp.zeros_like(acc_c)
@@ -342,14 +375,18 @@
             acc_s[j * DH:(j + 1) * DH, :] += squares
             acc_c[j * DH:(j + 1) * DH, :] += crosses
 
-    for n in range(2):
+    def mine(n):
         all_home(pin, pi_s, pi_r, n).wait_recv()
         settle(core == 0, pin, lpr, st, n)
         give(st, ps_s, ps_r, n, own0).start()
         loop(HG // PAIR, lambda r: inter(own0 + n * HG + r * PAIR))
-    for n in range(2):
+
+    def theirs(n):
         give(st, ps_s, ps_r, n, oth0).wait_recv()
         loop(HG // PAIR, lambda r: inter(oth0 + n * HG + r * PAIR))
+
+    loop(G, mine)
+    loop(G, theirs)
 
     pick = lax.broadcasted_iota(jnp.int32, (8, DH), 0) == 0
     for j in range(NJ):
@@ -365,11 +402,14 @@
         for j in range(NJ):
             sbf[h, j] = sbf[h, j].T
 
-    loop(H, turn)
-    for n in range(2):
+    units(0, U, turn)
+
+    def sent(n):
         all_out(rx, rx_s, rx_r, n).wait_send()
         all_back(pi_s, pi_r, n).wait_send()
         give(st, ps_s, ps_r, n, own0).wait_send()
+
+    loop(G, sent)
     hx_part = hx.at[pl.ds(0, NY - 1)]
     remote(hx_part, hx_part, hx_s.at[0], hx_r.at[0], mate).wait()
     for j in range(NJ):
@@ -393,8 +433,7 @@
             gain_part = gain_part + jnp.sum((grad * normed).reshape(DH // 8, 8, DH), axis=0)
             center = acc_c[j * DH:(j + 1) * DH, :]
             low = (inverse * (grad * scale - normed * center)).astype(BF16)
-            lifted = tile(ga, h, j).astype(F32) * jnp.exp(cum_row(h, j))
-            ms[h, j] = nn(lifted.astype(BF16), low)
+            ms[h, j] = nn(tile(ga, h, j), low)
             put(ga, h, j, low)
         ggp[h] = gain_part
         state = ms[h, NJ - 1]
@@ -403,13 +442,18 @@
             state = jnp.exp(end) * state + ms[h, j]
         loc[h] = state
 
-    for n in range(2):
-        loop(HG, lambda r: normalize(oth0 + n * HG + r))
+    def grads_mate(n):
+        heads(oth0 + n * HG, normalize)
         swap(loc, lpr, glp_s, glp_r, n).start()
-        loop(HG, lambda r: normalize(own0 + n * HG + r))
+
+    def grads_own(n):
+        heads(own0 + n * HG, normalize)
         swap(loc, lpr, glp_s, glp_r, n).wait()
         scan_total(core == 1, lpr, n)
         send_out(rx, grx_s, grx_r, n)
+
+    loop(G, grads_mate)
+    loop(G, grads_own)
 
     gain_copy = remote(ggp, ggpr, gp_s.at[0], gp_r.at[0], mate)
     gain_copy.start()
@@ -420,21 +464,25 @@
             cum = cums(h, j)
             decay = jnp.exp(jnp.where(lower, cum - cum_row(h, j), -jnp.inf))
             gw = (nn(gj, tile(kt, h, j)) * decay).astype(BF16)
-            gq = nn(gw, tile(k, h, j)) + jnp.exp(cum) * nn(gj, sbf[h, j])
+            grown = (gj.astype(F32) * jnp.exp(cum)).astype(BF16)
+            gq = nn(gw, tile(k, h, j)) + nn(grown, sbf[h, j])
             put(gvi, h, j, nn(tile(wt, h, j), gj))
             put(att, h, j, nn(gw.T, tile(q, h, j)))
             put(q, h, j, gq.astype(BF16))
 
-    loop(cut0, intra_grads)
+    soon = U // 8
+    units(0, soon, intra_grads)
     gain_copy.wait()
     ggc[...] = ggp[...] + ggpr[...]
     ggrx[chip] = ggc[chip]
-    prefix(rx, pin, grx_s, grx_r, 0, True)
-    send_back(pin, gpi_s, gpi_r, 0)
     others(lambda i: remote(ggc.at[i], ggrx.at[chip], gr_s.at[0], gr_r.at[0], at(i)).start())
-    loop(cut1 - cut0, lambda r: intra_grads(cut0 + r))
-    prefix(rx, pin, grx_s, grx_r, 1, True)
-    send_back(pin, gpi_s, gpi_r, 1)
+
+    def backward(n):
+        prefix(rx, pin, grx_s, grx_r, n, True)
+        send_back(pin, gpi_s, gpi_r, n)
+        units(soon + n, 1, intra_grads)
+
+    loop(G, backward)
     gr_part = ggrx.at[pl.ds(0, NC - 1)]
     remote(gr_part, gr_part, gr_s.at[0], gr_r.at[0], mate).wait()
     part = ggrx[0]
@@ -443,7 +491,7 @@
     ggsum[...] = part
     ggall[chip] = part
     others(lambda i: remote(ggsum, ggall.at[chip], ga_s.at[0], ga_r.at[0], at(i)).start())
-    loop(H - cut1, lambda r: intra_grads(cut1 + r))
+    units(soon + G, U - soon - G, intra_grads)
 
     def later_states(h):
         state = st[h]
@@ -456,23 +504,29 @@
         later_states(h)
         inter_grads(sizes, h, h, k, v, cb, sbf, att, gvi, k, v)
 
-    for n in range(2):
+    def last_mine(n):
         all_home(pin, gpi_s, gpi_r, n).wait_recv()
         settle(core == 1, pin, lpr, st, n)
         give(st, gps_s, gps_r, n, own0).start()
-        loop(HG, lambda r: own_grads(own0 + n * HG + r))
-    for n in range(2):
+        heads(own0 + n * HG, own_grads)
+
+    def last_theirs(n):
         give(st, gps_s, gps_r, n, oth0).wait_recv()
-        loop(HG, lambda r: later_states(oth0 + n * HG + r))
+        heads(oth0 + n * HG, later_states)
+
+    loop(G, last_mine)
+    loop(G, last_theirs)
 
     gg_part = ggall.at[pl.ds(0, NC - 1)]
     remote(gg_part, gg_part, ga_s.at[0], ga_r.at[0], mate).wait()
     for h in range(H):
         gg_out[h:h + 1, :] = jnp.sum(ggall[h], axis=0, keepdims=True)
-    for n in range(2):
+    def done(n):
         all_out(rx, grx_s, grx_r, n).wait_send()
         all_back(gpi_s, gpi_r, n).wait_send()
         give(st, gps_s, gps_r, n, own0).wait_send()
+
+    loop(G, done)
 
 
 def on_device(sizes, queries, key_rows, value_rows, log_decay, norm_gain, grad_out):
@@ -480,13 +534,14 @@
     W = H * DH
     NJ = T // DH
     HH = H // 2
-    HG = HH // 2
+    G = groups_of(HH)
+    HG = HH // G
     RS = HG * DH // NC
     V = pltpu.VMEM
     D = pltpu.SemaphoreType.DMA
-    rows = V((2, HG * DH, DH), F32)
-    slots = V((2, NC, RS, DH), F32)
-    heads = V((2, HG, DH, DH), F32)
+    rows = V((G, HG * DH, DH), F32)
+    slots = V((G, NC, RS, DH), F32)
+    heads = V((G, HG, DH, DH), F32)
     states = V((H, DH, DH), F32)
     scratch = [
         V((H, 1, T), F32), V((H, NJ, DH, DH), F32), V((T, W), BF16), V((T, W), BF16),
@@ -497,7 +552,7 @@
         states, rows, slots, heads, heads, slots, rows, states,
         V((H, 8, DH), F32), V((H, 8, DH), F32), V((H, 8, DH), F32), V((NC, 8, DH), F32),
         V((8, DH), F32), V((NC, 8, DH), F32),
-        D((4,)), *[D((1,))] * 6, *[D((2,))] * 16, *[D((1,))] * 6,
+        D((4,)), *[D((1,))] * 6, *[D((G,))] * 16, *[D((1,))] * 6,
     ]
     anywhere = pl.BlockSpec(memory_space=pl.ANY)
     local = pl.BlockSpec(memory_space=V)

time: 71.2 us -> 67.3 us (0.945)
  Pallas kernels: 70.4 us -> 66.3 us
    pallas_call x1, Pallas kernels: 65 us -> 61 us  [on_device(): pl.pallas_call(functools.partial(kernel, sizes), out_shape=held, in_specs...]
where the time goes in v4:
time: 67.3 us; the launch traced here: 67.1 us
  Pallas kernels  66.3 us (99%)
  between operations  0.8 us (1%)
    pallas_call x1, Pallas kernels, on_device(): pl.pallas_call(functools.partial(kernel, sizes), out_shape=held, in_specs...  61 us
    pallas_call x1, Pallas kernels, on_device(): pl.pallas_call(functools.partial(finish, sizes), out_shape=(big, big, big...  5.36 us

profile of v4, /device:TPU:1, one launch (start us, length us, event | category | flops | bytes accessed | tf_op | source)
XLA Modules:
  0.0 67.1 jit_solution(15030368565258133772)
XLA Ops:
  0.6 61.0 %shard_map.101 = (bf16[768,2048]{1,0:T(8,128)(2,1)S(1)}, bf16[768,2048]{1,0:T(8,128)(2,1)S(1)}, bf16[768,2048]{1,0:T(8,128)(2,1)S(1)}, bf16[768,2048]{1,0:T(8,12...) custom-call(bf16[768,2048]{1,0:T(8,128)(2,1)} %q_in.1, ...), custom_call_target="tpu_custom_call" | custom-call | tf_op jit(solution)/shard_map/pallas_call | solution.py:564
  61.6 5.4 %shard_map.102 = (bf16[768,2048]{1,0:T(8,128)(2,1)}, bf16[768,2048]{1,0:T(8,128)(2,1)}, bf16[768,2048]{1,0:T(8,128)(2,1)}, bf16[768,2048]{1,0:T(8,128)(2,1)}, f32[16,128]{1,0:T(8,128)}) custom-call(bf16[768,2048]{1,0:T(8,128)(2,1)S(1)} %get-tuple-element.19.q, bf16[768,2048]{1,0:T(8,128)(2,1)S(1)} %get-tuple-element.20.k, ...), custom_call_target="tpu_custom_call" | custom-call | tf_op jit(solution)/shard_map/pallas_call | solution.py:576

commit v5 on v4

--- a/solution.py
+++ b/solution.py
@@ -45,14 +45,14 @@
     ref[j * DH:(j + 1) * DH, pl.ds(pl.multiple_of(h * DH, DH), DH)] = value
 
 
-def inter_grads(sizes, h, to, k, v, cb, sbf, att, gvi, gk, gv):
+def inter_grads(sizes, h, k, v, cb, sbf, att, gvi, gk, gv):
     for j in range(sizes[0] // DH):
         cum = cb[h, j * DH:(j + 1) * DH, :]
         low = sbf[h, j]
         tail = jnp.exp(cum[DH - 1:DH, :] - cum)
         kj, vj = tile(k, h, j), tile(v, h, j)
-        put(gk, to, j, (tile(att, h, j) + tail * nn(vj, low.T)).astype(BF16))
-        put(gv, to, j, (tile(gvi, h, j) + tail * nn(kj, low)).astype(BF16))
+        put(gk, h, j, (tile(att, h, j) + tail * nn(vj, low.T)).astype(BF16))
+        put(gv, h, j, (tile(gvi, h, j) + tail * nn(kj, low)).astype(BF16))
 
 
 def finish(
@@ -61,39 +61,35 @@
     out_hbm, gq_hbm, gk_hbm, gv_hbm, gg_out,
     gk, gv, sem, head_sem,
 ):
-    HH = sizes[1] // 2
-    HW = HH * DH
-    core = lax.axis_index("seq") % 2
-    own = pl.ds(pl.multiple_of(core * HW, HW), HW)
+    H = sizes[1]
     copies = [
         pltpu.make_async_copy(src, dst, sem.at[n])
-        for n, (src, dst) in enumerate((
-            (g, out_hbm), (q, gq_hbm),
-            (k.at[:, own], gk_hbm.at[:, own]), (v.at[:, own], gv_hbm.at[:, own]),
-        ))
+        for n, (src, dst) in enumerate(((g, out_hbm), (q, gq_hbm)))
     ]
     for c in copies:
         c.start()
     gg_out[...] = gg[...]
 
-    def stores(r):
-        src = pl.ds(pl.multiple_of(r * DH, DH), DH)
-        dst = pl.ds(pl.multiple_of(((1 - core) * HH + r) * DH, DH), DH)
+    def stores(h):
+        columns = pl.ds(pl.multiple_of(h * DH, DH), DH)
         return [
-            pltpu.make_async_copy(a.at[:, src], b.at[:, dst], head_sem.at[n, r])
+            pltpu.make_async_copy(a.at[:, columns], b.at[:, columns], head_sem.at[n, h])
             for n, (a, b) in enumerate(((gk, gk_hbm), (gv, gv_hbm)))
         ]
 
-    def one(r, carry):
-        inter_grads(sizes, (1 - core) * HH + r, r, k, v, cb, sbf, att, gvi, gk, gv)
-        for c in stores(r):
+    def one(h, carry):
+        inter_grads(sizes, h, k, v, cb, sbf, att, gvi, gk, gv)
+        for c in stores(h):
             c.start()
         return carry
 
-    lax.fori_loop(0, HH, one, 0)
-    for r in range(HH):
-        for c in stores(r):
+    def ended(h, carry):
+        for c in stores(h):
             c.wait()
+        return carry
+
+    lax.fori_loop(0, H, one, 0)
+    lax.fori_loop(0, H, ended, 0)
     for c in copies:
         c.wait()
 
@@ -470,7 +466,7 @@
             put(att, h, j, nn(gw.T, tile(q, h, j)))
             put(q, h, j, gq.astype(BF16))
 
-    soon = U // 8
+    soon = U // 4
     units(0, soon, intra_grads)
     gain_copy.wait()
     ggc[...] = ggp[...] + ggpr[...]
@@ -480,9 +476,11 @@
     def backward(n):
         prefix(rx, pin, grx_s, grx_r, n, True)
         send_back(pin, gpi_s, gpi_r, n)
-        units(soon + n, 1, intra_grads)
-
-    loop(G, backward)
+
+    backward(0)
+    units(soon, 1, intra_grads)
+    span(1, G, backward)
+    units(soon + 1, U - soon - 2, intra_grads)
     gr_part = ggrx.at[pl.ds(0, NC - 1)]
     remote(gr_part, gr_part, gr_s.at[0], gr_r.at[0], mate).wait()
     part = ggrx[0]
@@ -491,7 +489,6 @@
     ggsum[...] = part
     ggall[chip] = part
     others(lambda i: remote(ggsum, ggall.at[chip], ga_s.at[0], ga_r.at[0], at(i)).start())
-    units(soon + G, U - soon - G, intra_grads)
 
     def later_states(h):
         state = st[h]
@@ -500,21 +497,18 @@
             if j > 0:
                 state = jnp.exp(cb[h, j * DH + DH - 1:j * DH + DH, :]) * state + ms[h, j]
 
-    def own_grads(h):
-        later_states(h)
-        inter_grads(sizes, h, h, k, v, cb, sbf, att, gvi, k, v)
-
     def last_mine(n):
         all_home(pin, gpi_s, gpi_r, n).wait_recv()
         settle(core == 1, pin, lpr, st, n)
         give(st, gps_s, gps_r, n, own0).start()
-        heads(own0 + n * HG, own_grads)
 
     def last_theirs(n):
         give(st, gps_s, gps_r, n, oth0).wait_recv()
         heads(oth0 + n * HG, later_states)
 
     loop(G, last_mine)
+    units(U - 1, 1, intra_grads)
+    loop(G, lambda n: heads(own0 + n * HG, later_states))
     loop(G, last_theirs)
 
     gg_part = ggall.at[pl.ds(0, NC - 1)]
@@ -579,9 +573,9 @@
         in_specs=[local] * len(held),
         out_specs=(anywhere, anywhere, anywhere, anywhere, local),
         scratch_shapes=[
-            V((T, W // 2), BF16), V((T, W // 2), BF16), D((4,)), D((2, HH)),
+            V((T, W), BF16), V((T, W), BF16), D((2,)), D((2, H)),
         ],
-        compiler_params=pltpu.CompilerParams(vmem_limit_bytes=5 << 20),
+        compiler_params=pltpu.CompilerParams(vmem_limit_bytes=9 << 20),
     )(*parts)
     return (*grads, gain_grad.reshape(W))
 

time: 67.3 us -> 65.9 us (0.979); the launches traced: 67.1 us -> 64.9 us
  Pallas kernels: 66.3 us -> 64.1 us
    pallas_call x1, Pallas kernels: 61 us -> 57.2 us  [on_device(): pl.pallas_call(functools.partial(kernel, sizes), out_shape=held, in_specs...]
    pallas_call x1, Pallas kernels: 5.36 us -> 6.81 us  [on_device(): pl.pallas_call(functools.partial(finish, sizes), out_shape=(big, big, big...]
where the time goes in v5:
time: 65.9 us; the launch traced here: 64.9 us
  Pallas kernels  64.1 us (97%)
  between operations  0.8 us (1%)
    pallas_call x1, Pallas kernels, on_device(): pl.pallas_call(functools.partial(kernel, sizes), out_shape=held, in_specs...  57.2 us
    pallas_call x1, Pallas kernels, on_device(): pl.pallas_call(functools.partial(finish, sizes), out_shape=(big, big, big...  6.81 us

profile of v5, /device:TPU:1, one launch (start us, length us, event | category | flops | bytes accessed | tf_op | source)
XLA Modules:
  0.0 64.9 jit_solution(12627260744312559616)
XLA Ops:
  0.6 57.2 %shard_map.101 = (bf16[768,2048]{1,0:T(8,128)(2,1)S(1)}, bf16[768,2048]{1,0:T(8,128)(2,1)S(1)}, bf16[768,2048]{1,0:T(8,128)(2,1)S(1)}, bf16[768,2048]{1,0:T(8,12...) custom-call(bf16[768,2048]{1,0:T(8,128)(2,1)} %q_in.1, ...), custom_call_target="tpu_custom_call" | custom-call | tf_op jit(solution)/shard_map/pallas_call | solution.py:558
  57.9 6.8 %shard_map.102 = (bf16[768,2048]{1,0:T(8,128)(2,1)}, bf16[768,2048]{1,0:T(8,128)(2,1)}, bf16[768,2048]{1,0:T(8,128)(2,1)}, bf16[768,2048]{1,0:T(8,128)(2,1)}, f32[16,128]{1,0:T(8,128)}) custom-call(bf16[768,2048]{1,0:T(8,128)(2,1)S(1)} %get-tuple-element.19.q, bf16[768,2048]{1,0:T(8,128)(2,1)S(1)} %get-tuple-element.20.k, ...), custom_call_target="tpu_custom_call" | custom-call | tf_op jit(solution)/shard_map/pallas_call | solution.py:570

commit v6 on v5

--- a/solution.py
+++ b/solution.py
@@ -156,12 +156,18 @@
     def others(body):
         lax.fori_loop(1, NC, lambda r, c: (body(lax.rem(chip + r, NC)), c)[1], 0)
 
+    near = pl.ds(pl.multiple_of(oth0 * DH, HH * DH), HH * DH)
+    late = pl.ds(pl.multiple_of(own0 * DH, HH * DH), HH * DH)
     loads = [
         pltpu.make_async_copy(src, dst, in_sem.at[n])
-        for n, (src, dst) in enumerate(((k_in, k), (v_in, v), (q_in, q), (g_in, g)))
+        for n, (src, dst) in enumerate((
+            (k_in.at[:, near], k.at[:, near]), (v_in.at[:, near], v.at[:, near]),
+            (k_in.at[:, late], k.at[:, late]), (v_in.at[:, late], v.at[:, late]),
+            (q_in, q), (g_in, g),
+        ))
     ]
-    loads[0].start()
-    loads[1].start()
+    for c in loads[:4]:
+        c.start()
 
     barrier = pltpu.get_barrier_semaphore()
     others(
@@ -182,14 +188,13 @@
     for j in range(NJ):
         piece = ld[:, j * DH:(j + 1) * DH]
         rows = exact_nt(piece, tri)
-        columns = exact_nt(tri, piece)
+        acc_c[j * DH:(j + 1) * DH, 0:H] = exact_nt(tri, piece)
         for h in range(H):
             rc[h, :, j * DH:(j + 1) * DH] = rows[h:h + 1, :]
-            cb[h, j * DH:(j + 1) * DH, :] = jnp.broadcast_to(columns[:, h:h + 1], (DH, DH))
         total = total + rows[:, DH - 1:DH]
     dec_own[...] = jnp.broadcast_to(total, (H, DH)).reshape(H, 1, DH)
-    loads[2].start()
-    loads[3].start()
+    for c in loads[4:]:
+        c.start()
 
     def cums(h, j):
         return cb[h, j * DH:(j + 1) * DH, :]
@@ -207,7 +212,7 @@
             scaled = (flipped.astype(F32) * jnp.exp(end - row)).astype(BF16)
             part = nn(scaled, tile(v, h, j))
             ms[h, j] = part
-            last = jnp.exp(cb[h, j * DH + DH - 1:j * DH + DH, :])
+            last = jnp.broadcast_to(jnp.exp(end), (1, DH))
             state = part if state is None else last * state + part
         loc[h] = state
 
@@ -321,9 +326,15 @@
         scan_total(core == 0, lpr, n)
         send_out(rx, rx_s, rx_r, n)
 
+    loads[2].wait()
+    loads[3].wait()
     loop(G, for_own)
-
-    loads[2].wait()
+    for j in range(NJ):
+        columns = acc_c[j * DH:(j + 1) * DH, 0:H]
+        for h in range(H):
+            cb[h, j * DH:(j + 1) * DH, :] = jnp.broadcast_to(columns[:, h:h + 1], (DH, DH))
+
+    loads[4].wait()
 
     def intra(h):
         for j in range(NJ):
@@ -347,7 +358,7 @@
 
     loop(G, forward)
     units(ahead + G, U - ahead - G, intra)
-    loads[3].wait()
+    loads[5].wait()
     acc_s[...] = jnp.zeros_like(acc_s)
     acc_c[...] = jnp.zeros_like(acc_c)
 
@@ -546,7 +557,7 @@
         states, rows, slots, heads, heads, slots, rows, states,
         V((H, 8, DH), F32), V((H, 8, DH), F32), V((H, 8, DH), F32), V((NC, 8, DH), F32),
         V((8, DH), F32), V((NC, 8, DH), F32),
-        D((4,)), *[D((1,))] * 6, *[D((G,))] * 16, *[D((1,))] * 6,
+        D((6,)), *[D((1,))] * 6, *[D((G,))] * 16, *[D((1,))] * 6,
     ]
     anywhere = pl.BlockSpec(memory_space=pl.ANY)
     local = pl.BlockSpec(memory_space=V)

time: 65.9 us -> 65.8 us (level)
  no operation moved by 1% of the time
where the time goes in v6:
time: 65.8 us; the launch traced here: 64.8 us
  Pallas kernels  64 us (97%)
  between operations  0.8 us (1%)
    pallas_call x1, Pallas kernels, on_device(): pl.pallas_call(functools.partial(kernel, sizes), out_shape=held, in_specs...  57.2 us
    pallas_call x1, Pallas kernels, on_device(): pl.pallas_call(functools.partial(finish, sizes), out_shape=(big, big, big...  6.81 us

profile of v6, /device:TPU:1, one launch (start us, length us, event | category | flops | bytes accessed | tf_op | source)
XLA Modules:
  0.0 64.8 jit_solution(4563723437195504521)
XLA Ops:
  0.6 57.2 %shard_map.101 = (bf16[768,2048]{1,0:T(8,128)(2,1)S(1)}, bf16[768,2048]{1,0:T(8,128)(2,1)S(1)}, bf16[768,2048]{1,0:T(8,128)(2,1)S(1)}, bf16[768,2048]{1,0:T(8,12...) custom-call(bf16[768,2048]{1,0:T(8,128)(2,1)} %q_in.1, ...), custom_call_target="tpu_custom_call" | custom-call | tf_op jit(solution)/shard_map/pallas_call | solution.py:569
  57.8 6.8 %shard_map.102 = (bf16[768,2048]{1,0:T(8,128)(2,1)}, bf16[768,2048]{1,0:T(8,128)(2,1)}, bf16[768,2048]{1,0:T(8,128)(2,1)}, bf16[768,2048]{1,0:T(8,128)(2,1)}, f32[16,128]{1,0:T(8,128)}) custom-call(bf16[768,2048]{1,0:T(8,128)(2,1)S(1)} %get-tuple-element.19.q, bf16[768,2048]{1,0:T(8,128)(2,1)S(1)} %get-tuple-element.20.k, ...), custom_call_target="tpu_custom_call" | custom-call | tf_op jit(solution)/shard_map/pallas_call | solution.py:581
